TPU v7x, 32 devices: a whole 2x2x4 slice. The times are simulated.
32 devices in a mesh: band: 8 (over z, y), ga: 4 (over x, core).
Axes of the slice: x: 2, y: 2, z: 4, core: 2. Of those that a mesh axis runs over, the one named last changes fastest.
Arguments:
- orbitals: float32 [8, 96, 9216], P('band', 'ga'), may hold values from -6 to 6
- retained: int32 [96, 9216], P(None, 'ga'), may hold values 0 or 1
Outputs:
- exchange_field: float32 [8, 96, 9216], P('band', 'ga')
- block_matrix: float32 [8, 1], P('band')
All inputs are finite; a program needn't handle non-finite values. No bound on the sum of `retained` on one device may be relied on, other than what follows from the above.
Results may differ from a plain program's by a relative error of at most 0.0086.
Values may be sent and summed in bfloat16 or wider, within the bound.
No kernel may reach another device: no remote copies, remote signals or barrier semaphores. Data moves between devices by JAX's collectives and lax.ppermute only.
A program may use at most 64 MiB of HBM per device.

v0:
```python
import math
from functools import partial

import jax
import jax.numpy as jnp
import numpy as np
from jax import lax
from jax.experimental import pallas as pl
from jax.experimental.pallas import tpu as pltpu
from jax.sharding import PartitionSpec as P

LANES = 128


def passed_along(value, axis, steps):
    count = lax.axis_size(axis)
    pairs = [(source, (source + steps) % count) for source in range(count)]
    return lax.ppermute(value, axis, pairs)


def cas_table(length):
    counter = np.arange(length)
    angles = 2.0 * np.pi / length * (counter[:, None] * counter[None, :] % length)
    scaled = (np.cos(angles) + np.sin(angles)) / np.sqrt(float(length))
    return scaled.astype(np.float32).astype(jnp.bfloat16).astype(np.float32)


def wrapped(indices, length):
    return jnp.where(indices < length // 2, indices, indices - length).astype(jnp.float32)


def screening(rows_x, rows_y, rows_z, length):
    freq_x = wrapped(rows_x, length)
    freq_y = wrapped(rows_y, length)
    freq_z = wrapped(rows_z, length)
    squared = freq_x[:, None, None] ** 2 + freq_y[None, :, None] ** 2 + freq_z[None, None, :] ** 2
    spread = length / 4.0
    return 1.0 / (1.0 + squared / (spread * spread))


def lane_of(shape):
    return lax.broadcasted_iota(jnp.int32, shape, len(shape) - 1)


def dense(parts, length):
    spill = LANES - length
    lane = lane_of(parts[0].shape)
    last = parts[-1]
    return [
        jnp.where(lane < length, part, pltpu.roll(last, (length - spill * j) % LANES, last.ndim - 1))
        for j, part in enumerate(parts[:-1])
    ]


def undense(parts, length):
    spill = LANES - length
    lane = lane_of(parts[0].shape)
    last = jnp.zeros_like(parts[0])
    for j, part in enumerate(parts):
        moved = pltpu.roll(part, (spill * j - length) % LANES, part.ndim - 1)
        last = jnp.where((lane >= spill * j) & (lane < spill * (j + 1)), moved, last)
    return last


def dot(a, b):
    return jnp.dot(a, b, preferred_element_type=jnp.float32)


class Sizes:
    def __init__(self, length, slab, groups, start, rows):
        self.length = length
        self.slab = slab
        self.start = start
        self.rows = rows
        self.groups = groups
        self.cols = length // groups
        whole = math.lcm(length, LANES)
        self.pack = whole // length
        self.chunks = whole // LANES
        self.quads = length // self.pack
        self.width = self.pack * length
        self.inner = rows // self.pack
        self.span = self.inner * self.cols
        assert self.chunks == self.pack - 1 and self.inner % 2 == 0 and self.cols % 2 == 0
        assert groups & (groups - 1) == 0


def tables(plans):
    sz = plans[0][0]
    table = cas_table(sz.length)
    spread = np.zeros((sz.width, sz.pack * LANES), np.float32)
    for r in range(sz.pack):
        spread[r * sz.length:(r + 1) * sz.length, r * LANES:r * LANES + sz.length] = table
    y_order = np.arange(sz.length).reshape(sz.quads, sz.pack).T.reshape(-1)
    turned = []
    for me in range(sz.groups):
        peers = np.arange(sz.groups) ^ me
        freq = np.arange(sz.length).reshape(sz.groups, sz.cols)[peers].reshape(-1)
        y = table[freq][:, y_order]
        found = [y, y.T]
        for plan in plans:
            x_order = []
            for cut in plan:
                inside = cut.start + np.arange(cut.rows).reshape(cut.pack, 1, cut.inner)
                x_order.append((inside + peers.reshape(1, -1, 1) * cut.slab).reshape(-1))
            x = table[:, np.concatenate(x_order)]
            found += [x, x.T]
        turned.append(np.stack(found))
    turned = jnp.asarray(np.stack(turned), jnp.bfloat16)
    mine = lax.dynamic_index_in_dim(turned, lax.axis_index("ga"), 0, keepdims=False)
    return jnp.asarray(spread, jnp.bfloat16), jnp.asarray(spread.T, jnp.bfloat16), mine


def pieces(row):
    rows, rest = [], row
    for _ in range(3):
        rows.append(rest.astype(jnp.bfloat16).astype(jnp.float32))
        rest = rest - rows[-1]
    at = lax.broadcasted_iota(jnp.int32, (8, LANES), 0)
    out = jnp.zeros((8, LANES), jnp.float32)
    for i, piece in enumerate(rows):
        out = jnp.where(at == i, piece, out)
    return out


def forward_kernel(sz, a_ref, b_ref, z_ref, t_ref, *refs):
    out_refs, s_ref = refs[:-1], refs[-1]
    w = sz.width
    rows = jnp.concatenate(
        [
            a_ref[sz.start:sz.start + sz.rows, q * w:(q + 1) * w]
            * b_ref[:, q * w:(q + 1) * w].astype(jnp.float32)
            for q in range(sz.quads)
        ],
        axis=0,
    ).astype(jnp.bfloat16)
    spread = dot(rows, z_ref[...])
    for r in range(sz.pack):
        s_ref[r] = spread[:, r * LANES:(r + 1) * LANES]
    y = t_ref[0]
    for xi in range(0, sz.inner, 2):
        planes = []
        for g in range(sz.pack):
            col = jnp.concatenate(
                [
                    jnp.concatenate(
                        [
                            s_ref[r, pl.ds(g * sz.inner + xi + h, sz.quads, stride=sz.rows), :]
                            for r in range(sz.pack)
                        ],
                        axis=0,
                    )
                    for h in range(2)
                ],
                axis=1,
            ).astype(jnp.bfloat16)
            planes.append(dot(y, col))
        packed = [
            dense([plane[:, h * LANES:(h + 1) * LANES] for plane in planes], sz.length)
            for h in range(2)
        ]
        for j in range(sz.chunks):
            for p in range(sz.groups):
                cut = slice(p * sz.cols, (p + 1) * sz.cols)
                out_refs[p][j, xi * sz.cols:(xi + 2) * sz.cols, :] = jnp.concatenate(
                    [packed[0][j][cut], packed[1][j][cut]], axis=0
                ).astype(jnp.bfloat16)


def middle_kernel(plan, which, *refs):
    sz, n, count = plan[0], plan[0].groups, len(plan)
    r_refs, refs = refs[:n * count], refs[n * count:]
    (t_ref, screen_ref), refs = refs[:2], refs[2:]
    out_refs, refs = refs[:n * count], refs[n * count:]
    f_refs, g_refs = refs[:count], refs[count:]
    for c, cut in enumerate(plan):
        for s in range(n):
            parts = [r_refs[c * n + s][j].astype(jnp.float32) for j in range(sz.chunks)]
            for g, part in enumerate(parts + [undense(parts, sz.length)]):
                f_refs[c][g, s * cut.span:(s + 1) * cut.span, :] = part
    total = jnp.zeros((sz.length, LANES), jnp.float32)
    x, xb = t_ref[2 + 2 * which], t_ref[3 + 2 * which]
    for ky in range(0, sz.cols, 2):
        col = jnp.concatenate(
            [
                jnp.concatenate(
                    [
                        f_refs[c][g, pl.ds(ky + h, n * cut.inner, stride=sz.cols), :]
                        for c, cut in enumerate(plan)
                        for g in range(sz.pack)
                    ],
                    axis=0,
                )
                for h in range(2)
            ],
            axis=1,
        ).astype(jnp.bfloat16)
        spectrum = dot(x, col).astype(jnp.bfloat16).astype(jnp.float32)
        screen = jnp.concatenate([screen_ref[ky], screen_ref[ky + 1]], axis=1)
        weighted = spectrum * screen
        energy = spectrum * weighted
        total = total + energy[:, :LANES] + energy[:, LANES:]
        back = dot(xb, weighted.astype(jnp.bfloat16))
        for h in range(2):
            at = 0
            for c, cut in enumerate(plan):
                many = n * cut.inner
                for g in range(sz.pack):
                    g_refs[c][g, pl.ds(ky + h, many, stride=sz.cols), :] = back[
                        at:at + many, h * LANES:(h + 1) * LANES
                    ]
                    at += many
    tail = pieces(jnp.sum(total, axis=0, keepdims=True))
    tail = jnp.concatenate([tail, jnp.zeros_like(tail)], axis=0).astype(jnp.bfloat16)
    for c, cut in enumerate(plan):
        for s in range(n):
            parts = [g_refs[c][g, s * cut.span:(s + 1) * cut.span, :] for g in range(sz.pack)]
            out_ref = out_refs[c * n + s]
            for j, part in enumerate(dense(parts, sz.length)):
                out_ref[j * cut.span:(j + 1) * cut.span, :] = part.astype(jnp.bfloat16)
            if cut.start == 0:
                out_ref[sz.chunks * cut.span:, :] = tail


def backward_body(sz, r_refs, zb_ref, t_ref, s_ref):
    span = sz.inner * sz.cols
    yb = t_ref[1]
    for xi in range(0, sz.inner, 2):
        blocks = []
        for p in range(sz.groups):
            parts = [
                r_refs[p][j * span + xi * sz.cols:j * span + (xi + 2) * sz.cols, :].astype(jnp.float32)
                for j in range(sz.chunks)
            ]
            blocks.append(parts + [undense(parts, sz.length)])
        for g in range(sz.pack):
            col = jnp.concatenate(
                [
                    jnp.concatenate(
                        [blocks[p][g][h * sz.cols:(h + 1) * sz.cols] for p in range(sz.groups)],
                        axis=0,
                    )
                    for h in range(2)
                ],
                axis=1,
            ).astype(jnp.bfloat16)
            plane = dot(yb, col)
            for h in range(2):
                for r in range(sz.pack):
                    s_ref[r, pl.ds(g * sz.inner + xi + h, sz.quads, stride=sz.rows), :] = plane[
                        r * sz.quads:(r + 1) * sz.quads, h * LANES:(h + 1) * LANES
                    ]
    total = None
    if sz.start == 0:
        total = sum(
            jnp.sum(r_refs[p][sz.chunks * span:, :].astype(jnp.float32), axis=0, keepdims=True)
            for p in range(sz.groups)
        )
    rows = jnp.concatenate([s_ref[r].astype(jnp.bfloat16) for r in range(sz.pack)], axis=1)
    return dot(rows, zb_ref[...]).astype(jnp.bfloat16).astype(jnp.float32), total


def own_kernel(sz, plan, *refs):
    n = sz.groups
    r_refs, refs = refs[:n], refs[n:]
    part_refs, refs = refs[:len(plan)], refs[len(plan):]
    a_ref, sum_in_ref, zb_ref, t_ref, out_ref, sum_ref, s_ref = refs
    v, total = backward_body(sz, r_refs, zb_ref, t_ref, s_ref)
    sum_ref[...] = total + sum_in_ref[...]
    for q in range(sz.quads):
        lanes = slice(q * sz.width, (q + 1) * sz.width)
        own = v[q * sz.rows:(q + 1) * sz.rows]
        for cut, part_ref in zip(plan, part_refs):
            rows = slice(cut.start, cut.start + cut.rows)
            out_ref[rows, lanes] = own[rows] * a_ref[rows, lanes] + part_ref[:, lanes]


def cross_kernel(sz, again, *refs):
    n = sz.groups
    first = sz.start == 0
    r_refs, refs = refs[:n], refs[n:]
    a_ref, b_ref, zb_ref, t_ref = refs[:4]
    refs = refs[4:]
    if again:
        run_ref, carry_ref = refs[:2]
        refs = refs[2:]
        if first:
            sum_in_ref, refs = refs[0], refs[1:]
    out_ref, back_ref, s_ref = refs[0], refs[1], refs[-1]
    v, total = backward_body(sz, r_refs, zb_ref, t_ref, s_ref)
    cells = a_ref.shape[1]
    rows = slice(sz.start, sz.start + sz.rows)
    for q in range(sz.quads):
        lanes = slice(q * sz.width, (q + 1) * sz.width)
        part = v[q * sz.rows:(q + 1) * sz.rows]
        out = part * b_ref[:, lanes].astype(jnp.float32)
        back = part * a_ref[rows, lanes]
        if again:
            out = out + run_ref[:, lanes]
            back = back + carry_ref[:, lanes].astype(jnp.float32)
        out_ref[:, lanes] = out
        back_ref[:, lanes] = back.astype(back_ref.dtype)
    if first:
        sum_ref = refs[2]
        sum_ref[...] = total + sum_in_ref[...] if again else total
        if again:
            carried = carry_ref[:, cells:].astype(jnp.float32)
            total = total + jnp.sum(carried, axis=0, keepdims=True)
        tail = pieces(total)
        if sz.rows > tail.shape[0]:
            rest = jnp.zeros((sz.rows - tail.shape[0], LANES), jnp.float32)
            tail = jnp.concatenate([tail, rest], axis=0)
        back_ref[:, cells:] = tail.astype(back_ref.dtype)


def last_kernel(sz, plan, run_ref, sum_ref, *refs):
    got_refs, (out_ref, block_ref) = refs[:len(plan)], refs[len(plan):]
    cells = run_ref.shape[1]
    total = sum_ref[...]
    for cut, got_ref in zip(plan, got_refs):
        rows = slice(cut.start, cut.start + cut.rows)
        out_ref[rows] = run_ref[rows] + got_ref[:, :cells].astype(jnp.float32)
        if cut.start == 0:
            carried = got_ref[:, cells:].astype(jnp.float32)
            total = total + jnp.sum(carried, axis=0, keepdims=True)
    block_ref[...] = jnp.sum(total, axis=1, keepdims=True) / float(sz.length**3)


def call(kernel, outs, args, scratch=()):
    held = [pltpu.with_memory_space_constraint(arg, pltpu.VMEM) for arg in args]
    return pl.pallas_call(
        kernel,
        out_shape=[pltpu.VMEM(shape, kind) for shape, kind in outs],
        in_specs=[pl.BlockSpec(memory_space=pltpu.VMEM)] * len(args),
        out_specs=[pl.BlockSpec(memory_space=pltpu.VMEM)] * len(outs),
        scratch_shapes=list(scratch),
        compiler_params=pltpu.CompilerParams(vmem_limit_bytes=24 * 2**20),
    )(*held)


def after(value, before):
    return value if before is None else lax.optimization_barrier((value, before))[0]


def exchange(blocks):
    count = len(blocks)
    got = {0: blocks[0]}
    for k in range(count - 1, 0, -1):
        got[k] = lax.ppermute(blocks[k], "ga", [(d, d ^ k) for d in range(count)])
    return [got[k] for k in range(count)]


def chunk_rows(rows):
    least = 8
    return [rows - least, least] if rows > least else [rows]


def local(orbitals, retained):
    bands_dev, slab_rows, plane_cells = orbitals.shape
    assert bands_dev == 1
    length = retained.shape[0]
    groups = lax.axis_size("ga")
    sz = Sizes(length, slab_rows, groups, 0, slab_rows)
    plan, at = [], 0
    for rows in chunk_rows(slab_rows):
        plan.append(Sizes(length, slab_rows, groups, at, rows))
        at += rows
    z, zb, mine = tables([[sz], plan])
    lattice = orbitals.reshape(slab_rows, plane_cells)
    half, full = jnp.bfloat16, jnp.float32
    counter = jnp.arange(length, dtype=jnp.int32)
    local_y = lax.axis_index("ga") * sz.cols + jnp.arange(sz.cols, dtype=jnp.int32)
    screen = screening(counter, local_y, counter, length) * retained.reshape(
        length, sz.cols, length
    ).astype(jnp.float32)
    screen = jnp.pad(screen.transpose(1, 0, 2), ((0, 0), (0, 0), (0, LANES - length)))

    flat = (slab_rows, plane_cells)

    def lines(cut):
        return pltpu.VMEM((cut.pack, cut.quads * cut.rows, LANES), full)

    def mids(cut):
        return pltpu.VMEM((cut.pack, groups * cut.span, LANES), full)

    def forward(cut, visitors):
        there = [((cut.chunks, cut.span, LANES), half)] * groups
        kernel = partial(forward_kernel, cut)
        return call(kernel, there, [lattice, visitors, z, mine], [lines(cut)])

    def middle(cuts, which, got):
        outs = []
        for cut in cuts:
            tail = 16 if cut.start == 0 else 0
            outs += [((cut.chunks * cut.span + tail, LANES), half)] * groups
        scratch = [mids(cut) for cut in cuts] * 2
        kernel = partial(middle_kernel, cuts, which)
        sent = call(kernel, outs, got + [mine, screen], scratch)
        return [sent[c * groups:(c + 1) * groups] for c in range(len(cuts))]

    def crossed(cut, got, visitors, old):
        first = cut.start == 0
        outs = [
            ((cut.rows, plane_cells), full),
            ((cut.rows, plane_cells + (LANES if first else 0)), half),
        ]
        if first:
            outs.append(((1, LANES), full))
        kernel = partial(cross_kernel, cut, len(old) > 0)
        return call(kernel, outs, got + [lattice, visitors, zb, mine] + old, [lines(cut)])

    def pair(visitors, old, ahead=None):
        got, before = [], None
        for c, cut in enumerate(plan):
            before = forward(cut, after(visitors[c], before))
            got += exchange(before)
        got = after(got, ahead)
        sent = middle(plan, 1, got)
        fresh = [None] * len(plan)
        for c in reversed(range(len(plan))):
            fresh[c] = crossed(plan[c], exchange(sent[c]), visitors[c], old[c])
        return [part[0] for part in fresh], [part[1] for part in fresh], fresh[0][2]

    band_reach = max(1, lax.axis_size("band") // 8)
    visitors = []
    for cut in plan:
        chunk = lattice[cut.start:cut.start + cut.rows].astype(half)
        visitors.append(passed_along(chunk, "band", 1))
    sent = forward(sz, lattice)
    visitors = [after(chunk, sent) for chunk in visitors]
    sent = middle([sz], 0, exchange(sent))[0]
    running, carried, total = pair(visitors, [[]] * len(plan), sent)

    def round_once(rounds_done, state):
        visitors, running, carried, total = state
        visitors = [passed_along(chunk, "band", 1) for chunk in visitors]
        carried = [passed_along(chunk, "band", 1) for chunk in carried]
        old = [list(both) for both in zip(running, carried)]
        old[0].append(total)
        running, carried, total = pair(visitors, old)
        return visitors, running, carried, total

    if band_reach > 1:
        state = (visitors, running, carried, total)
        visitors, running, carried, total = lax.fori_loop(1, band_reach, round_once, state)
    returned = []
    for chunk in carried:
        returned.append(passed_along(chunk, "band", -band_reach))
    sent = after(sent, total)
    running, total = call(
        partial(own_kernel, sz, plan),
        [(flat, full), ((1, LANES), full)],
        exchange(sent) + running + [lattice, total, zb, mine],
        [lines(sz)],
    )
    field, block = pl.pallas_call(
        partial(last_kernel, sz, plan),
        out_shape=[jax.ShapeDtypeStruct(flat, full), jax.ShapeDtypeStruct((1, 1), full)],
        compiler_params=pltpu.CompilerParams(vmem_limit_bytes=24 * 2**20),
        name="last",
    )(*[pltpu.with_memory_space_constraint(v, pltpu.VMEM) for v in [running, total] + returned])
    return field.reshape(orbitals.shape), block


def solution(mesh):
    placed = (P("band", "ga", None), P(None, "ga"))

    return jax.shard_map(
        local,
        mesh=mesh,
        in_specs=placed,
        out_specs=(P("band", "ga", None), P("band", None)),
        check_vma=False,
    )
```

profile of v0, /device:TPU:0, one launch (start us, length us, event | category | flops | bytes accessed | tf_op | source)
XLA Modules:
  0.0 62.8 jit_solution(15804097333496885708)
XLA Ops:
  0.6 0.9 %dynamic-slice_bitcast_fusion.t_ref.refs_4_.refs_8_.refs_7_.refs_9_ = bf16[6,96,96]{2,1,0:T(8,128)(2,1)S(1)} fusion(bf16[4,6,96,96]{3,2,1,0:T(8,128)(2,1)} %constant.34.clone, s32[]{:T(128)S(6)} %select_n.27), kind=kLoop, calls=%fused_computation.4 | loop fusion | bytes 221188 | tf_op jit(solution)/shard_map/jit(dynamic_index_in_dim)/squeeze | solution.py:110
  1.6 0.0 copy-start
  1.6 1.2 %copy-done = f32[1,24,9216]{2,1,0:T(8,128)S(1)} copy-done((f32[1,24,9216]{2,1,0:T(8,128)S(1)}, f32[1,24,9216]{2,1,0:T(8,128)}, u32[]{:S(2)}) %copy-start) | copy-done | bytes 884760
  2.7 1.0 %copy-done.2 = bf16[384,512]{1,0:T(8,128)(2,1)S(1)} copy-done((bf16[384,512]{1,0:T(8,128)(2,1)S(1)}, bf16[384,512]{1,0:T(8,128)(2,1)}, u32[]{:S(2)}) %copy-start.2) | copy-done | bytes 393240
  3.7 0.9 %shard_map.68 = (bf16[3,144,128]{2,1,0:T(8,128)(2,1)S(1)}, bf16[3,144,128]{2,1,0:T(8,128)(2,1)S(1)}, bf16[3,144,128]{2,1,0:T(8,128)(2,1)S(1)}, bf16[3,144,128]{2,1,0:T(8,128)(2,1)S(1)}) custom-call(f32[24,9216]{1,0:T(8,128)S(1)} %bitcast.10, f32[24,9216]{1,0:T(8,128)S(1)} %bitcast.11, bf16[384,512]{1,0:T(8,128)(2,1)S(1)} %copy-done.2, ...), custom_call_target="tpu_custom_call" | custom-call | tf_op jit(solution)/shard_map/pallas_call | solution.py:331
  4.6 0.0 copy-start.1
  4.7 0.0 copy-start.3
  4.7 0.6 collective-permute-start
  5.2 2.5 %collective-permute-start.1 = (bf16[3,144,128]{2,1,0:T(8,128)(2,1)S(1)}, bf16[3,144,128]{2,1,0:T(8,128)(2,1)S(1)}, u32[]{:S(2)}, u32[]{:S(2)}) collective-permute-start(bf16[3,144,128]{2,1,0:T(8,128)(2,1)S(1)} %get-tuple-element.52), channel_id=1, source_target_pairs={{0,2},{1,3},{2,0},{3,1},{4,6},{5,7},{6,4},{7,5},{8,10},{9,11},{10,... | collective-permute-start | bytes 331784 | tf_op jit(solution)/shard_map/ppermute | solution.py:349
  7.8 0.0 collective-permute-start.2
  7.9 1.8 %collective-permute-start.3 = (bf16[16,9216]{1,0:T(8,128)(2,1)S(1)}, bf16[16,9216]{1,0:T(8,128)(2,1)S(1)}, u32[]{:S(2)}, u32[]{:S(2)}) collective-permute-start(bf16[16,9216]{1,0:T(8,128)(2,1)S(1)} %slice_bitcast_fusion), channel_id=1, source_target_pairs={{0,4},{4,8},{8,12},{12,16},{16,20},{20,24},{24,28},{28,0},{1,5},{5... | collective-permute-start | bytes 884744 | tf_op jit(solution)/shard_map/ppermute | solution.py:18
  9.7 1.6 %collective-permute-start.7 = (bf16[8,9216]{1,0:T(8,128)(2,1)S(1)}, bf16[8,9216]{1,0:T(8,128)(2,1)S(1)}, u32[]{:S(2)}, u32[]{:S(2)}) collective-permute-start(bf16[8,9216]{1,0:T(8,128)(2,1)S(1)} %slice_bitcast_fusion.1), channel_id=1, source_target_pairs={{0,4},{4,8},{8,12},{12,16},{16,20},{20,24},{24,28},{28,0},{1,5},{5... | collective-permute-start | bytes 442376 | tf_op jit(solution)/shard_map/ppermute | solution.py:18
  11.3 12.1 %collective-permute-done.7.b_ref.refs_5_ = bf16[8,9216]{1,0:T(8,128)(2,1)S(1)} collective-permute-done((bf16[8,9216]{1,0:T(8,128)(2,1)S(1)}, bf16[8,9216]{1,0:T(8,128)(2,1)S(1)}, u32[]{:S(2)}, u32[]{:S(2)}) %collective-permute-start.7) | collective-permute-done | bytes 147488 | tf_op jit(solution)/shard_map/ppermute | solution.py:18
  23.5 0.0 collective-permute-done.3.b_ref.refs_5_
  23.5 0.8 %shard_map.70 = (bf16[3,96,128]{2,1,0:T(8,128)(2,1)S(1)}, bf16[3,96,128]{2,1,0:T(8,128)(2,1)S(1)}, bf16[3,96,128]{2,1,0:T(8,128)(2,1)S(1)}, bf16[3,96,128]{2,1,0:T(8,128)(2,1)S(1)}) custom-call(f32[24,9216]{1,0:T(8,128)S(1)} %bitcast.12, bf16[16,9216]{1,0:T(8,128)(2,1)S(1)} %collective-permute-done.3.b_ref.refs_5_, bf16[384,512]{1,0:T(8,128)(2,1)S(1)} %copy-done.3, ...), custom_call_target="tpu_custom_call" | custom-call | tf_op jit(solution)/shard_map/pallas_call | solution.py:331
  24.3 0.0 copy-start.5
  24.3 0.6 shard_map.71
  24.9 0.1 collective-permute-start.8
  25.0 0.1 broadcast_add_fusion
  25.1 0.4 copy-done.5
  25.5 1.0 %convert_element_type.39 = f32[96,2304]{1,0:T(8,128)} convert(s32[96,2304]{1,0:T(8,128)S(1)} %copy-done.5) | non-fusion elementwise | flops 221184 | bytes 1769472 | tf_op jit(solution)/shard_map/convert_element_type | solution.py:375
  26.5 3.0 %convert_element_type.40 = f32[96,24,96]{2,1,0:T(8,128)} reshape(f32[96,2304]{1,0:T(8,128)} %convert_element_type.39) | data formatting | bytes 1769472 | tf_op jit(solution)/shard_map/convert_element_type | solution.py:375
  29.4 0.1 collective-permute-start.4
  29.5 0.0 collective-permute-done.refs_1_
  29.5 1.5 %collective-permute-start.5 = (bf16[3,96,128]{2,1,0:T(8,128)(2,1)S(1)}, bf16[3,96,128]{2,1,0:T(8,128)(2,1)S(1)}, u32[]{:S(2)}, u32[]{:S(2)}) collective-permute-start(bf16[3,96,128]{2,1,0:T(8,128)(2,1)S(1)} %get-tuple-element.61), channel_id=1, source_target_pairs={{0,2},{1,3},{2,0},{3,1},{4,6},{5,7},{6,4},{7,5},{8,10},{9,11},{10,... | collective-permute-start | bytes 221192 | tf_op jit(solution)/shard_map/ppermute | solution.py:349
  31.0 0.0 collective-permute-done.1.refs_2_
  31.0 0.3 collective-permute-start.6
  31.3 0.0 collective-permute-done.2.refs_3_
  31.3 1.5 %collective-permute-start.9 = (bf16[3,48,128]{2,1,0:T(8,128)(2,1)S(1)}, bf16[3,48,128]{2,1,0:T(8,128)(2,1)S(1)}, u32[]{:S(2)}, u32[]{:S(2)}) collective-permute-start(bf16[3,48,128]{2,1,0:T(8,128)(2,1)S(1)} %get-tuple-element.67), channel_id=1, source_target_pairs={{0,2},{1,3},{2,0},{3,1},{4,6},{5,7},{6,4},{7,5},{8,10},{9,11},{10,... | collective-permute-start | bytes 110600 | tf_op jit(solution)/shard_map/ppermute | solution.py:349
  32.8 0.2 collective-permute-start.10
  33.0 1.7 %fusion = f32[24,96,96]{2,1,0:T(8,128)S(1)} fusion(f32[96,24,96]{2,1,0:T(8,128)} %convert_element_type.40, f32[96]{0:T(128)S(1)} %fusion.2, f32[96,24]{0,1:T(8,128)S(1)} %broadcast_add_fusion), kind=kLoop, calls=%fused_computation.1 | loop fusion | flops 1105920 | bytes 1779072 | tf_op jit(solution)/shard_map/transpose | solution.py:376
  34.7 0.1 pad.4.refs_5_.refs_9_
  34.8 0.9 %shard_map.69 = (bf16[448,128]{1,0:T(8,128)(2,1)S(1)}, bf16[448,128]{1,0:T(8,128)(2,1)S(1)}, bf16[448,128]{1,0:T(8,128)(2,1)S(1)}, bf16[448,128]{1,0:T(8,128)(2,1)S(1)}) custom-call(bf16[3,144,128]{2,1,0:T(8,128)(2,1)S(1)} %get-tuple-element.50.refs_0_, bf16[3,144,128]{2,1,0:T(8,128)(2,1)S(1)} %collective-permute-done.refs_1_, ...), custom_call_target="tpu_custom_call" | custom-call | tf_op jit(solution)/shard_map/pallas_call | solution.py:331
  35.7 0.0 copy-start.4
  35.7 1.0 %collective-permute-done.9.refs_6_ = bf16[3,48,128]{2,1,0:T(8,128)(2,1)S(1)} collective-permute-done((bf16[3,48,128]{2,1,0:T(8,128)(2,1)S(1)}, bf16[3,48,128]{2,1,0:T(8,128)(2,1)S(1)}, u32[]{:S(2)}, u32[]{:S(2)}) %collective-permute-start.9) | collective-permute-done | bytes 36896 | tf_op jit(solution)/shard_map/ppermute | solution.py:349
  36.7 0.4 collective-permute-done.10.refs_7_
  37.1 0.0 collective-permute-done.4.refs_1_
  37.1 0.0 collective-permute-done.5.refs_2_
  37.1 0.0 collective-permute-done.6.refs_3_
  37.1 0.9 %shard_map.72 = (bf16[304,128]{1,0:T(8,128)(2,1)S(1)}, bf16[304,128]{1,0:T(8,128)(2,1)S(1)}, bf16[304,128]{1,0:T(8,128)(2,1)S(1)}, bf16[304,128]{1,0:T(8,128)(2,...) custom-call(bf16[3,96,128]{2,1,0:T(8,128)(2,1)S(1)} %get-tuple-eleme, ...), custom_call_target="tpu_custom_call" | custom-call | tf_op jit(solution)/shard_map/pallas_call | solution.py:331
  38.0 0.2 collective-permute-start.11
  38.2 1.4 %collective-permute-start.12 = (bf16[304,128]{1,0:T(8,128)(2,1)S(1)}, bf16[304,128]{1,0:T(8,128)(2,1)S(1)}, u32[]{:S(2)}, u32[]{:S(2)}) collective-permute-start(bf16[304,128]{1,0:T(8,128)(2,1)S(1)} %get-tuple-element.79), channel_id=1, source_target_pairs={{0,2},{1,3},{2,0},{3,1},{4,6},{5,7},{6,4},{7,5},{8,10},{9,11},{10,... | collective-permute-start | bytes 233480 | tf_op jit(solution)/shard_map/ppermute | solution.py:349
  39.5 0.4 collective-permute-start.13
  39.9 0.0 collective-permute-done.11.refs_1_
  39.9 3.2 %collective-permute-done.12.refs_2_ = bf16[304,128]{1,0:T(8,128)(2,1)S(1)} collective-permute-done((bf16[304,128]{1,0:T(8,128)(2,1)S(1)}, bf16[304,128]{1,0:T(8,128)(2,1)S(1)}, u32[]{:S(2)}, u32[]{:S(2)}) %collective-permute-start.12) | collective-permute-done | bytes 77856 | tf_op jit(solution)/shard_map/ppermute | solution.py:349
  43.1 1.1 %collective-permute-done.13.refs_3_ = bf16[304,128]{1,0:T(8,128)(2,1)S(1)} collective-permute-done((bf16[304,128]{1,0:T(8,128)(2,1)S(1)}, bf16[304,128]{1,0:T(8,128)(2,1)S(1)}, u32[]{:S(2)}, u32[]{:S(2)}) %collective-permute-start.13) | collective-permute-done | bytes 77856 | tf_op jit(solution)/shard_map/ppermute | solution.py:349
  44.2 0.7 %shard_map.73 = (f32[16,9216]{1,0:T(8,128)S(1)}, bf16[16,9344]{1,0:T(8,128)(2,1)S(1)}, f32[1,128]{1,0:T(1,128)S(1)}) custom-call(bf16[304,128]{1,0:T(8,128)(2,1)S(1)} %get-tuple-element.77.refs_0_, bf16[304,128]{1,0:T(8,128)(2,1)S(1)} %collective-permute-done.11.refs_1_, bf16[304,128]{1,0:T(8,128)(2,1)S(1)} %collective-permute-done.12.refs_2_, ...), custom_call_target="tpu_custom_call" | custom-call | tf_op jit(solution)/shard_map/pallas_call | solution.py:331
  44.9 1.8 %collective-permute-start.20 = (bf16[16,9344]{1,0:T(8,128)(2,1)S(1)}, bf16[16,9344]{1,0:T(8,128)(2,1)S(1)}, u32[]{:S(2)}, u32[]{:S(2)}) collective-permute-start(bf16[16,9344]{1,0:T(8,128)(2,1)S(1)} %get-tuple-element.94), channel_id=1, source_target_pairs={{0,28},{4,0},{8,4},{12,8},{16,12},{20,16},{24,20},{28,24},{1,29},{... | collective-permute-start | bytes 897032 | tf_op jit(solution)/shard_map/ppermute | solution.py:18
  46.7 0.0 collective-permute-start.17
  46.7 1.1 %collective-permute-start.18 = (bf16[144,128]{1,0:T(8,128)(2,1)S(1)}, bf16[144,128]{1,0:T(8,128)(2,1)S(1)}, u32[]{:S(2)}, u32[]{:S(2)}) collective-permute-start(bf16[144,128]{1,0:T(8,128)(2,1)S(1)} %get-tuple-element.89), channel_id=1, source_target_pairs={{0,2},{1,3},{2,0},{3,1},{4,6},{5,7},{6,4},{7,5},{8,10},{9,11},{10,... | collective-permute-start | bytes 110600 | tf_op jit(solution)/shard_map/ppermute | solution.py:349
  47.9 0.7 %collective-permute-start.19 = (bf16[144,128]{1,0:T(8,128)(2,1)S(1)}, bf16[144,128]{1,0:T(8,128)(2,1)S(1)}, u32[]{:S(2)}, u32[]{:S(2)}) collective-permute-start(bf16[144,128]{1,0:T(8,128)(2,1)S(1)} %get-tuple-element.90), channel_id=1, source_target_pairs={{0,3},{1,2},{2,1},{3,0},{4,7},{5,6},{6,5},{7,4},{8,11},{9,10},{10,... | collective-permute-start | bytes 110600 | tf_op jit(solution)/shard_map/ppermute | solution.py:349
  48.6 0.0 collective-permute-done.17.refs_1_
  48.6 2.1 %collective-permute-done.18.refs_2_ = bf16[144,128]{1,0:T(8,128)(2,1)S(1)} collective-permute-done((bf16[144,128]{1,0:T(8,128)(2,1)S(1)}, bf16[144,128]{1,0:T(8,128)(2,1)S(1)}, u32[]{:S(2)}, u32[]{:S(2)}) %collective-permute-start.18) | collective-permute-done | bytes 36896 | tf_op jit(solution)/shard_map/ppermute | solution.py:349
  50.7 0.7 %collective-permute-done.19.refs_3_ = bf16[144,128]{1,0:T(8,128)(2,1)S(1)} collective-permute-done((bf16[144,128]{1,0:T(8,128)(2,1)S(1)}, bf16[144,128]{1,0:T(8,128)(2,1)S(1)}, u32[]{:S(2)}, u32[]{:S(2)}) %collective-permute-start.19) | collective-permute-done | bytes 36896 | tf_op jit(solution)/shard_map/ppermute | solution.py:349
  51.4 0.5 shard_map.74
  51.9 1.5 %collective-permute-start.21 = (bf16[8,9216]{1,0:T(8,128)(2,1)S(1)}, bf16[8,9216]{1,0:T(8,128)(2,1)S(1)}, u32[]{:S(2)}, u32[]{:S(2)}) collective-permute-start(bf16[8,9216]{1,0:T(8,128)(2,1)S(1)} %get-tuple-element.95), channel_id=1, source_target_pairs={{0,28},{4,0},{8,4},{12,8},{16,12},{20,16},{24,20},{28,24},{1,29},{... | collective-permute-start | bytes 442376 | tf_op jit(solution)/shard_map/ppermute | solution.py:18
  53.4 0.0 collective-permute-start.14
  53.4 1.0 %collective-permute-start.15 = (bf16[448,128]{1,0:T(8,128)(2,1)S(1)}, bf16[448,128]{1,0:T(8,128)(2,1)S(1)}, u32[]{:S(2)}, u32[]{:S(2)}) collective-permute-start(bf16[448,128]{1,0:T(8,128)(2,1)S(1)} %get-tuple-element.84), channel_id=1, source_target_pairs={{0,2},{1,3},{2,0},{3,1},{4,6},{5,7},{6,4},{7,5},{8,10},{9,11},{10,... | collective-permute-start | bytes 344072 | tf_op jit(solution)/shard_map/ppermute | solution.py:349
  54.4 0.8 %collective-permute-start.16 = (bf16[448,128]{1,0:T(8,128)(2,1)S(1)}, bf16[448,128]{1,0:T(8,128)(2,1)S(1)}, u32[]{:S(2)}, u32[]{:S(2)}) collective-permute-start(bf16[448,128]{1,0:T(8,128)(2,1)S(1)} %get-tuple-element.85), channel_id=1, source_target_pairs={{0,3},{1,2},{2,1},{3,0},{4,7},{5,6},{6,5},{7,4},{8,11},{9,10},{10,... | collective-permute-start | bytes 344072 | tf_op jit(solution)/shard_map/ppermute | solution.py:349
  55.3 4.2 %collective-permute-done.15.refs_2_ = bf16[448,128]{1,0:T(8,128)(2,1)S(1)} collective-permute-done((bf16[448,128]{1,0:T(8,128)(2,1)S(1)}, bf16[448,128]{1,0:T(8,128)(2,1)S(1)}, u32[]{:S(2)}, u32[]{:S(2)}) %collective-permute-start.15) | collective-permute-done | bytes 114720 | tf_op jit(solution)/shard_map/ppermute | solution.py:349
  59.5 1.5 %collective-permute-done.16.refs_3_ = bf16[448,128]{1,0:T(8,128)(2,1)S(1)} collective-permute-done((bf16[448,128]{1,0:T(8,128)(2,1)S(1)}, bf16[448,128]{1,0:T(8,128)(2,1)S(1)}, u32[]{:S(2)}, u32[]{:S(2)}) %collective-permute-start.16) | collective-permute-done | bytes 114720 | tf_op jit(solution)/shard_map/ppermute | solution.py:349
  60.9 0.8 %shard_map.75 = (f32[24,9216]{1,0:T(8,128)S(1)}, f32[1,128]{1,0:T(1,128)S(1)}) custom-call(bf16[448,128]{1,0:T(8,128)(2,1)S(1)} %get-tuple-element.82.refs_0_, bf16[448,128]{1,0:T(8,128)(2,1)S(1)} %collective-permute-done.14.refs_1_, bf16[448,128]{1,0:T(8,128)(2,1)S(1)} %collective-permute-done.15.refs_2_, ...), custom_call_target="tpu_custom_call" | custom-call | tf_op jit(solution)/shard_map/pallas_call | solution.py:331
  61.7 0.0 collective-permute-done.21.refs_1_
  61.8 1.0 %last.1 = (f32[24,9216]{1,0:T(8,128)}, f32[1,1]{1,0:T(1,128)}) custom-call(f32[24,9216]{1,0:T(8,128)S(1)} %get-tuple-element.92.run_ref, f32[1,128]{1,0:T(1,128)S(1)} %get-tuple-element.93.sum_ref, bf16[16,9344]{1,0:T(8,128)(2,1)S(1)} %collective-permute-done.20.refs_0_, bf16[8,9216]{1,0:T(8,128)(2,1)S(1)} %collective-permute-done.21.refs_1_), custom_call_target="tpu_custom_call" | custom-call | tf_op jit(solution)/shard_map/last/pallas_call | solution.py:456
  (12 shorter events, 0.1 us)
Async XLA Ops:
  1.6 1.2 %copy-start = (f32[1,24,9216]{2,1,0:T(8,128)S(1)}, f32[1,24,9216]{2,1,0:T(8,128)}, u32[]{:S(2)}) copy-start(f32[1,24,9216]{2,1,0:T(8,128)} %param.5) | copy-start | bytes 2654212
  2.7 1.0 %copy-start.2 = (bf16[384,512]{1,0:T(8,128)(2,1)S(1)}, bf16[384,512]{1,0:T(8,128)(2,1)}, u32[]{:S(2)}) copy-start(bf16[384,512]{1,0:T(8,128)(2,1)} %constant.35.clone.z_ref) | copy-start | bytes 1179652
  4.6 18.8 %copy-start.1 = (f32[1,24,9216]{2,1,0:T(8,128)S(1)}, f32[1,24,9216]{2,1,0:T(8,128)}, u32[]{:S(2)}) copy-start(f32[1,24,9216]{2,1,0:T(8,128)} %param.5) | copy-start | bytes 2654212
  4.7 18.8 %copy-start.3 = (bf16[384,512]{1,0:T(8,128)(2,1)S(1)}, bf16[384,512]{1,0:T(8,128)(2,1)}, u32[]{:S(2)}) copy-start(bf16[384,512]{1,0:T(8,128)(2,1)} %constant.35.clone.z_ref) | copy-start | bytes 1179652
  4.7 24.9 %collective-permute-start = (bf16[3,144,128]{2,1,0:T(8,128)(2,1)S(1)}, bf16[3,144,128]{2,1,0:T(8,128)(2,1)S(1)}, u32[]{:S(2)}, u32[]{:S(2)}) collective-permute-start(bf16[3,144,128]{2,1,0:T(8,128)(2,1)S(1)} %get-tuple-element.51), channel_id=1, source_target_pairs={{0,1},{1,0},{2,3},{3,2},{4,5},{5,4},{6,7},{7,6},{8,9},{9,8},{10,11... | collective-permute-start | bytes 331784 | tf_op jit(solution)/shard_map/ppermute | solution.py:349
  5.2 25.8 %collective-permute-start.1 = (bf16[3,144,128]{2,1,0:T(8,128)(2,1)S(1)}, bf16[3,144,128]{2,1,0:T(8,128)(2,1)S(1)}, u32[]{:S(2)}, u32[]{:S(2)}) collective-permute-start(bf16[3,144,128]{2,1,0:T(8,128)(2,1)S(1)} %get-tuple-element.52), channel_id=1, source_target_pairs={{0,2},{1,3},{2,0},{3,1},{4,6},{5,7},{6,4},{7,5},{8,10},{9,11},{10,... | collective-permute-start | bytes 331784 | tf_op jit(solution)/shard_map/ppermute | solution.py:349
  7.8 23.5 %collective-permute-start.2 = (bf16[3,144,128]{2,1,0:T(8,128)(2,1)S(1)}, bf16[3,144,128]{2,1,0:T(8,128)(2,1)S(1)}, u32[]{:S(2)}, u32[]{:S(2)}) collective-permute-start(bf16[3,144,128]{2,1,0:T(8,128)(2,1)S(1)} %get-tuple-element.53), channel_id=1, source_target_pairs={{0,3},{1,2},{2,1},{3,0},{4,7},{5,6},{6,5},{7,4},{8,11},{9,10},{10,... | collective-permute-start | bytes 331784 | tf_op jit(solution)/shard_map/ppermute | solution.py:349
  7.9 15.6 %collective-permute-start.3 = (bf16[16,9216]{1,0:T(8,128)(2,1)S(1)}, bf16[16,9216]{1,0:T(8,128)(2,1)S(1)}, u32[]{:S(2)}, u32[]{:S(2)}) collective-permute-start(bf16[16,9216]{1,0:T(8,128)(2,1)S(1)} %slice_bitcast_fusion), channel_id=1, source_target_pairs={{0,4},{4,8},{8,12},{12,16},{16,20},{20,24},{24,28},{28,0},{1,5},{5... | collective-permute-start | bytes 884744 | tf_op jit(solution)/shard_map/ppermute | solution.py:18
  9.7 13.7 %collective-permute-start.7 = (bf16[8,9216]{1,0:T(8,128)(2,1)S(1)}, bf16[8,9216]{1,0:T(8,128)(2,1)S(1)}, u32[]{:S(2)}, u32[]{:S(2)}) collective-permute-start(bf16[8,9216]{1,0:T(8,128)(2,1)S(1)} %slice_bitcast_fusion.1), channel_id=1, source_target_pairs={{0,4},{4,8},{8,12},{12,16},{16,20},{20,24},{24,28},{28,0},{1,5},{5... | collective-permute-start | bytes 442376 | tf_op jit(solution)/shard_map/ppermute | solution.py:18
  24.3 1.2 %copy-start.5 = (s32[96,2304]{1,0:T(8,128)S(1)}, s32[96,2304]{1,0:T(8,128)}, u32[]{:S(2)}) copy-start(s32[96,2304]{1,0:T(8,128)} %param.6) | copy-start | bytes 2654212
  24.9 7.9 %collective-permute-start.8 = (bf16[3,48,128]{2,1,0:T(8,128)(2,1)S(1)}, bf16[3,48,128]{2,1,0:T(8,128)(2,1)S(1)}, u32[]{:S(2)}, u32[]{:S(2)}) collective-permute-start(bf16[3,48,128]{2,1,0:T(8,128)(2,1)S(1)} %get-tuple-element.66), channel_id=1, source_target_pairs={{0,1},{1,0},{2,3},{3,2},{4,5},{5,4},{6,7},{7,6},{8,9},{9,8},{10,11... | collective-permute-start | bytes 110600 | tf_op jit(solution)/shard_map/ppermute | solution.py:349
  29.4 7.6 %collective-permute-start.4 = (bf16[3,96,128]{2,1,0:T(8,128)(2,1)S(1)}, bf16[3,96,128]{2,1,0:T(8,128)(2,1)S(1)}, u32[]{:S(2)}, u32[]{:S(2)}) collective-permute-start(bf16[3,96,128]{2,1,0:T(8,128)(2,1)S(1)} %get-tuple-element.60), channel_id=1, source_target_pairs={{0,1},{1,0},{2,3},{3,2},{4,5},{5,4},{6,7},{7,6},{8,9},{9,8},{10,11... | collective-permute-start | bytes 221192 | tf_op jit(solution)/shard_map/ppermute | solution.py:349
  29.5 7.6 %collective-permute-start.5 = (bf16[3,96,128]{2,1,0:T(8,128)(2,1)S(1)}, bf16[3,96,128]{2,1,0:T(8,128)(2,1)S(1)}, u32[]{:S(2)}, u32[]{:S(2)}) collective-permute-start(bf16[3,96,128]{2,1,0:T(8,128)(2,1)S(1)} %get-tuple-element.61), channel_id=1, source_target_pairs={{0,2},{1,3},{2,0},{3,1},{4,6},{5,7},{6,4},{7,5},{8,10},{9,11},{10,... | collective-permute-start | bytes 221192 | tf_op jit(solution)/shard_map/ppermute | solution.py:349
  31.0 6.1 %collective-permute-start.6 = (bf16[3,96,128]{2,1,0:T(8,128)(2,1)S(1)}, bf16[3,96,128]{2,1,0:T(8,128)(2,1)S(1)}, u32[]{:S(2)}, u32[]{:S(2)}) collective-permute-start(bf16[3,96,128]{2,1,0:T(8,128)(2,1)S(1)} %get-tuple-element.62), channel_id=1, source_target_pairs={{0,3},{1,2},{2,1},{3,0},{4,7},{5,6},{6,5},{7,4},{8,11},{9,10},{10,... | collective-permute-start | bytes 221192 | tf_op jit(solution)/shard_map/ppermute | solution.py:349
  31.3 5.4 %collective-permute-start.9 = (bf16[3,48,128]{2,1,0:T(8,128)(2,1)S(1)}, bf16[3,48,128]{2,1,0:T(8,128)(2,1)S(1)}, u32[]{:S(2)}, u32[]{:S(2)}) collective-permute-start(bf16[3,48,128]{2,1,0:T(8,128)(2,1)S(1)} %get-tuple-element.67), channel_id=1, source_target_pairs={{0,2},{1,3},{2,0},{3,1},{4,6},{5,7},{6,4},{7,5},{8,10},{9,11},{10,... | collective-permute-start | bytes 110600 | tf_op jit(solution)/shard_map/ppermute | solution.py:349
  32.8 4.3 %collective-permute-start.10 = (bf16[3,48,128]{2,1,0:T(8,128)(2,1)S(1)}, bf16[3,48,128]{2,1,0:T(8,128)(2,1)S(1)}, u32[]{:S(2)}, u32[]{:S(2)}) collective-permute-start(bf16[3,48,128]{2,1,0:T(8,128)(2,1)S(1)} %get-tuple-element.68), channel_id=1, source_target_pairs={{0,3},{1,2},{2,1},{3,0},{4,7},{5,6},{6,5},{7,4},{8,11},{9,10},{10,... | collective-permute-start | bytes 110600 | tf_op jit(solution)/shard_map/ppermute | solution.py:349
  35.7 8.5 %copy-start.4 = (bf16[512,384]{1,0:T(8,128)(2,1)S(1)}, bf16[512,384]{1,0:T(8,128)(2,1)}, u32[]{:S(2)}) copy-start(bf16[512,384]{1,0:T(8,128)(2,1)} %constant.36.clone.refs_6_.refs_8_) | copy-start | bytes 1179652
  38.0 1.9 %collective-permute-start.11 = (bf16[304,128]{1,0:T(8,128)(2,1)S(1)}, bf16[304,128]{1,0:T(8,128)(2,1)S(1)}, u32[]{:S(2)}, u32[]{:S(2)}) collective-permute-start(bf16[304,128]{1,0:T(8,128)(2,1)S(1)} %get-tuple-element.78), channel_id=1, source_target_pairs={{0,1},{1,0},{2,3},{3,2},{4,5},{5,4},{6,7},{7,6},{8,9},{9,8},{10,11... | collective-permute-start | bytes 233480 | tf_op jit(solution)/shard_map/ppermute | solution.py:349
  38.2 4.9 %collective-permute-start.12 = (bf16[304,128]{1,0:T(8,128)(2,1)S(1)}, bf16[304,128]{1,0:T(8,128)(2,1)S(1)}, u32[]{:S(2)}, u32[]{:S(2)}) collective-permute-start(bf16[304,128]{1,0:T(8,128)(2,1)S(1)} %get-tuple-element.79), channel_id=1, source_target_pairs={{0,2},{1,3},{2,0},{3,1},{4,6},{5,7},{6,4},{7,5},{8,10},{9,11},{10,... | collective-permute-start | bytes 233480 | tf_op jit(solution)/shard_map/ppermute | solution.py:349
  39.5 4.7 %collective-permute-start.13 = (bf16[304,128]{1,0:T(8,128)(2,1)S(1)}, bf16[304,128]{1,0:T(8,128)(2,1)S(1)}, u32[]{:S(2)}, u32[]{:S(2)}) collective-permute-start(bf16[304,128]{1,0:T(8,128)(2,1)S(1)} %get-tuple-element.80), channel_id=1, source_target_pairs={{0,3},{1,2},{2,1},{3,0},{4,7},{5,6},{6,5},{7,4},{8,11},{9,10},{10,... | collective-permute-start | bytes 233480 | tf_op jit(solution)/shard_map/ppermute | solution.py:349
  44.9 16.8 %collective-permute-start.20 = (bf16[16,9344]{1,0:T(8,128)(2,1)S(1)}, bf16[16,9344]{1,0:T(8,128)(2,1)S(1)}, u32[]{:S(2)}, u32[]{:S(2)}) collective-permute-start(bf16[16,9344]{1,0:T(8,128)(2,1)S(1)} %get-tuple-element.94), channel_id=1, source_target_pairs={{0,28},{4,0},{8,4},{12,8},{16,12},{20,16},{24,20},{28,24},{1,29},{... | collective-permute-start | bytes 897032 | tf_op jit(solution)/shard_map/ppermute | solution.py:18
  46.7 1.9 %collective-permute-start.17 = (bf16[144,128]{1,0:T(8,128)(2,1)S(1)}, bf16[144,128]{1,0:T(8,128)(2,1)S(1)}, u32[]{:S(2)}, u32[]{:S(2)}) collective-permute-start(bf16[144,128]{1,0:T(8,128)(2,1)S(1)} %get-tuple-element.88), channel_id=1, source_target_pairs={{0,1},{1,0},{2,3},{3,2},{4,5},{5,4},{6,7},{7,6},{8,9},{9,8},{10,11... | collective-permute-start | bytes 110600 | tf_op jit(solution)/shard_map/ppermute | solution.py:349
  46.7 4.0 %collective-permute-start.18 = (bf16[144,128]{1,0:T(8,128)(2,1)S(1)}, bf16[144,128]{1,0:T(8,128)(2,1)S(1)}, u32[]{:S(2)}, u32[]{:S(2)}) collective-permute-start(bf16[144,128]{1,0:T(8,128)(2,1)S(1)} %get-tuple-element.89), channel_id=1, source_target_pairs={{0,2},{1,3},{2,0},{3,1},{4,6},{5,7},{6,4},{7,5},{8,10},{9,11},{10,... | collective-permute-start | bytes 110600 | tf_op jit(solution)/shard_map/ppermute | solution.py:349
  47.9 3.6 %collective-permute-start.19 = (bf16[144,128]{1,0:T(8,128)(2,1)S(1)}, bf16[144,128]{1,0:T(8,128)(2,1)S(1)}, u32[]{:S(2)}, u32[]{:S(2)}) collective-permute-start(bf16[144,128]{1,0:T(8,128)(2,1)S(1)} %get-tuple-element.90), channel_id=1, source_target_pairs={{0,3},{1,2},{2,1},{3,0},{4,7},{5,6},{6,5},{7,4},{8,11},{9,10},{10,... | collective-permute-start | bytes 110600 | tf_op jit(solution)/shard_map/ppermute | solution.py:349
  51.9 9.8 %collective-permute-start.21 = (bf16[8,9216]{1,0:T(8,128)(2,1)S(1)}, bf16[8,9216]{1,0:T(8,128)(2,1)S(1)}, u32[]{:S(2)}, u32[]{:S(2)}) collective-permute-start(bf16[8,9216]{1,0:T(8,128)(2,1)S(1)} %get-tuple-element.95), channel_id=1, source_target_pairs={{0,28},{4,0},{8,4},{12,8},{16,12},{20,16},{24,20},{28,24},{1,29},{... | collective-permute-start | bytes 442376 | tf_op jit(solution)/shard_map/ppermute | solution.py:18
  53.4 1.9 %collective-permute-start.14 = (bf16[448,128]{1,0:T(8,128)(2,1)S(1)}, bf16[448,128]{1,0:T(8,128)(2,1)S(1)}, u32[]{:S(2)}, u32[]{:S(2)}) collective-permute-start(bf16[448,128]{1,0:T(8,128)(2,1)S(1)} %get-tuple-element.83), channel_id=1, source_target_pairs={{0,1},{1,0},{2,3},{3,2},{4,5},{5,4},{6,7},{7,6},{8,9},{9,8},{10,11... | collective-permute-start | bytes 344072 | tf_op jit(solution)/shard_map/ppermute | solution.py:349
  53.4 6.0 %collective-permute-start.15 = (bf16[448,128]{1,0:T(8,128)(2,1)S(1)}, bf16[448,128]{1,0:T(8,128)(2,1)S(1)}, u32[]{:S(2)}, u32[]{:S(2)}) collective-permute-start(bf16[448,128]{1,0:T(8,128)(2,1)S(1)} %get-tuple-element.84), channel_id=1, source_target_pairs={{0,2},{1,3},{2,0},{3,1},{4,6},{5,7},{6,4},{7,5},{8,10},{9,11},{10,... | collective-permute-start | bytes 344072 | tf_op jit(solution)/shard_map/ppermute | solution.py:349
  54.4 6.5 %collective-permute-start.16 = (bf16[448,128]{1,0:T(8,128)(2,1)S(1)}, bf16[448,128]{1,0:T(8,128)(2,1)S(1)}, u32[]{:S(2)}, u32[]{:S(2)}) collective-permute-start(bf16[448,128]{1,0:T(8,128)(2,1)S(1)} %get-tuple-element.85), channel_id=1, source_target_pairs={{0,3},{1,2},{2,1},{3,0},{4,7},{5,6},{6,5},{7,4},{8,11},{9,10},{10,... | collective-permute-start | bytes 344072 | tf_op jit(solution)/shard_map/ppermute | solution.py:349
where the time goes:
time: 63.1 us; the launch traced here: 62.8 us
  waiting for transfers between devices  26.3 us (42%)
  starting transfers between devices  19.1 us (30%)
  Pallas kernels  7.13 us (11%)
  local copies, waits for them, and re-layouts  6.64 us (11%)
  other arithmetic  2.76 us (4%)
  between operations  0.82 us (1%)
    ppermute x18, waiting for transfers between devices, exchange(): got[k] = lax.ppermute(blocks[k], 'ga', [(d, d ^ k) for d in range(count)])  14.2 us
    ppermute x18, starting transfers between devices, exchange(): got[k] = lax.ppermute(blocks[k], 'ga', [(d, d ^ k) for d in range(count)])  12.4 us
    ppermute x4, waiting for transfers between devices, passed_along(): return lax.ppermute(value, axis, pairs)  12.1 us
    ppermute x4, starting transfers between devices, passed_along(): return lax.ppermute(value, axis, pairs)  6.66 us
    pallas_call x8, Pallas kernels, call(): pl.pallas_call(kernel, out_shape=[pltpu.VMEM(shape, kind) for shape, kind...  6.11 us
    convert_element_type x1, local copies, waits for them, and re-layouts, local(): screen = screening(counter, local_y, counter, length) * retained.reshape(...  3 us
    unnamed x12, local copies, waits for them, and re-layouts  2.6 us
    transpose x1, other arithmetic, local(): screen.transpose(1, 0, 2)  1.66 us
  transfers between devices with their start and end apart: 22, of which 9 were waited for; matrix products, arithmetic and copies ran while one was open for 9% of the time, Pallas kernels for 6%

commit v1 on v0

--- a/solution.py
+++ b/solution.py
@@ -27,15 +27,6 @@
 
 def wrapped(indices, length):
     return jnp.where(indices < length // 2, indices, indices - length).astype(jnp.float32)
-
-
-def screening(rows_x, rows_y, rows_z, length):
-    freq_x = wrapped(rows_x, length)
-    freq_y = wrapped(rows_y, length)
-    freq_z = wrapped(rows_z, length)
-    squared = freq_x[:, None, None] ** 2 + freq_y[None, :, None] ** 2 + freq_z[None, None, :] ** 2
-    spread = length / 4.0
-    return 1.0 / (1.0 + squared / (spread * spread))
 
 
 def lane_of(shape):
@@ -121,6 +112,32 @@
     for i, piece in enumerate(rows):
         out = jnp.where(at == i, piece, out)
     return out
+
+
+def split_kernel(plan, a_ref, *out_refs):
+    for cut, out_ref in zip(plan, out_refs):
+        out_ref[...] = a_ref[cut.start:cut.start + cut.rows, :].astype(out_ref.dtype)
+
+
+def screen_kernel(sz, kept_ref, y_ref, out_ref):
+    shape = (sz.length, LANES)
+    lane = lane_of(shape)
+    freq_x = wrapped(lax.broadcasted_iota(jnp.int32, shape, 0), sz.length)
+    freq_z = wrapped(lane, sz.length)
+    plane_x, plane_z = freq_x * freq_x, freq_z * freq_z
+    spread = sz.length / 4.0
+    for ky in range(sz.cols):
+        at, off = divmod(ky * sz.length, LANES)
+        turn = (LANES - off) % LANES
+        kept = kept_ref[:, at * LANES:(at + 1) * LANES].astype(jnp.float32)
+        if turn:
+            kept = pltpu.roll(kept, turn, 1)
+        if off + sz.length > LANES:
+            more = kept_ref[:, (at + 1) * LANES:(at + 2) * LANES].astype(jnp.float32)
+            kept = jnp.where(lane < LANES - off, kept, pltpu.roll(more, turn, 1))
+        squared = plane_x + y_ref[ky] + plane_z
+        screen = 1.0 / (1.0 + squared / (spread * spread)) * kept
+        out_ref[ky] = jnp.where(lane < sz.length, screen, 0.0)
 
 
 def forward_kernel(sz, a_ref, b_ref, z_ref, t_ref, *refs):
@@ -368,12 +385,8 @@
     z, zb, mine = tables([[sz], plan])
     lattice = orbitals.reshape(slab_rows, plane_cells)
     half, full = jnp.bfloat16, jnp.float32
-    counter = jnp.arange(length, dtype=jnp.int32)
     local_y = lax.axis_index("ga") * sz.cols + jnp.arange(sz.cols, dtype=jnp.int32)
-    screen = screening(counter, local_y, counter, length) * retained.reshape(
-        length, sz.cols, length
-    ).astype(jnp.float32)
-    screen = jnp.pad(screen.transpose(1, 0, 2), ((0, 0), (0, 0), (0, LANES - length)))
+    local_y = jnp.broadcast_to((wrapped(local_y, length) ** 2)[:, None, None], (sz.cols, 1, LANES))
 
     flat = (slab_rows, plane_cells)
 
@@ -423,9 +436,14 @@
 
     band_reach = max(1, lax.axis_size("band") // 8)
     visitors = []
-    for cut in plan:
-        chunk = lattice[cut.start:cut.start + cut.rows].astype(half)
+    halves = call(
+        partial(split_kernel, plan), [((cut.rows, plane_cells), half) for cut in plan], [lattice]
+    )
+    for chunk in halves:
         visitors.append(passed_along(chunk, "band", 1))
+    screen = call(
+        partial(screen_kernel, sz), [((sz.cols, length, LANES), full)], [retained, local_y]
+    )[0]
     sent = forward(sz, lattice)
     visitors = [after(chunk, sent) for chunk in visitors]
     sent = middle([sz], 0, exchange(sent))[0]
@@ -446,7 +464,6 @@
     returned = []
     for chunk in carried:
         returned.append(passed_along(chunk, "band", -band_reach))
-    sent = after(sent, total)
     running, total = call(
         partial(own_kernel, sz, plan),
         [(flat, full), ((1, LANES), full)],

time: 63.1 us -> 54.4 us (0.86)
  waiting for transfers between devices: 26.3 us -> 22 us
  local copies, waits for them, and re-layouts: 6.64 us -> 3.77 us
  other arithmetic: 2.76 us -> 0.01 us
  Pallas kernels: 7.13 us -> 8.2 us
    ppermute x4, waiting for transfers between devices: 12.1 us -> 6.93 us  [passed_along(): return lax.ppermute(value, axis, pairs)]
    convert_element_type x3 -> x0, local copies, waits for them, and re-layouts: 3.03 us -> none  [the longest x1 3 us: local(): screen = screening(counter, local_y, counter, length) * retained.reshape(...]
    transpose x1 -> x0, other arithmetic: 1.66 us -> none  [local(): screen.transpose(1, 0, 2)]
    ppermute x4, starting transfers between devices: 6.66 us -> 7.82 us  [passed_along(): return lax.ppermute(value, axis, pairs)]
    pallas_call x8 -> x10, Pallas kernels: 6.11 us -> 7.18 us  [call(): pl.pallas_call(kernel, out_shape=[pltpu.VMEM(shape, kind) for shape, kind...]
    convert_element_type x1 -> x0, other arithmetic: 0.97 us -> none  [local(): screen = screening(counter, local_y, counter, length) * retained.reshape(...]
    ppermute x18, waiting for transfers between devices: 14.2 us -> 15.1 us  [exchange(): got[k] = lax.ppermute(blocks[k], 'ga', [(d, d ^ k) for d in range(count)])]
    ppermute x18, starting transfers between devices: 12.4 us -> 11.6 us  [exchange(): got[k] = lax.ppermute(blocks[k], 'ga', [(d, d ^ k) for d in range(count)])]
  transfers between devices with their start and end apart: 22 -> 22, of which waited for: 9 -> 9; matrix products, arithmetic and copies ran while one was open for 9% -> 2% of each run, Pallas kernels for 6% -> 10%
where the time goes in v1:
time: 54.4 us; the launch traced here: 54.2 us
  waiting for transfers between devices  22 us (40%)
  starting transfers between devices  19.4 us (36%)
  Pallas kernels  8.2 us (15%)
  local copies, waits for them, and re-layouts  3.77 us (7%)
  between operations  0.81 us (1%)
    ppermute x18, waiting for transfers between devices, exchange(): got[k] = lax.ppermute(blocks[k], 'ga', [(d, d ^ k) for d in range(count)])  15.1 us
    ppermute x18, starting transfers between devices, exchange(): got[k] = lax.ppermute(blocks[k], 'ga', [(d, d ^ k) for d in range(count)])  11.6 us
    ppermute x4, starting transfers between devices, passed_along(): return lax.ppermute(value, axis, pairs)  7.82 us
    pallas_call x10, Pallas kernels, call(): pl.pallas_call(kernel, out_shape=[pltpu.VMEM(shape, kind) for shape, kind...  7.18 us
    ppermute x4, waiting for transfers between devices, passed_along(): return lax.ppermute(value, axis, pairs)  6.93 us
    unnamed x12, local copies, waits for them, and re-layouts  2.77 us
  transfers between devices with their start and end apart: 22, of which 9 were waited for; matrix products, arithmetic and copies ran while one was open for 2% of the time, Pallas kernels for 10%

profile of v1, /device:TPU:0, one launch (start us, length us, event | category | flops | bytes accessed | tf_op | source)
XLA Modules:
  0.0 54.2 jit_solution(4637542356734095871)
XLA Ops:
  0.6 1.2 %copy-done = f32[1,24,9216]{2,1,0:T(8,128)S(1)} copy-done((f32[1,24,9216]{2,1,0:T(8,128)S(1)}, f32[1,24,9216]{2,1,0:T(8,128)}, u32[]{:S(2)}) %copy-start) | copy-done | bytes 884760
  1.8 3.0 %collective-permute-start.6 = (bf16[16,9216]{1,0:T(8,128)(2,1)S(1)}, bf16[16,9216]{1,0:T(8,128)(2,1)S(1)}, u32[]{:S(2)}, u32[]{:S(2)}) collective-permute-start(bf16[16,9216]{1,0:T(8,128)(2,1)S(1)} %get-tuple-element.56), channel_id=1, source_target_pairs={{0,4},{4,8},{8,12},{12,16},{16,20},{20,24},{24,28},{28,0},{1,5},{5... | collective-permute-start | bytes 884744 | tf_op jit(solution)/shard_map/ppermute | solution.py:18
  4.9 1.5 %collective-permute-start.10 = (bf16[8,9216]{1,0:T(8,128)(2,1)S(1)}, bf16[8,9216]{1,0:T(8,128)(2,1)S(1)}, u32[]{:S(2)}, u32[]{:S(2)}) collective-permute-start(bf16[8,9216]{1,0:T(8,128)(2,1)S(1)} %get-tuple-element.62), channel_id=1, source_target_pairs={{0,4},{4,8},{8,12},{12,16},{16,20},{20,24},{24,28},{28,0},{1,5},{5... | collective-permute-start | bytes 442376 | tf_op jit(solution)/shard_map/ppermute | solution.py:18
  6.4 0.9 %dynamic-slice_bitcast_fusion.t_ref.refs_4_.refs_8_.refs_7_.refs_9_ = bf16[6,96,96]{2,1,0:T(8,128)(2,1)S(1)} fusion(bf16[4,6,96,96]{3,2,1,0:T(8,128)(2,1)} %constant.23.clone, s32[]{:T(128)S(6)} %select_n.12), kind=kLoop, calls=%fused_computation | loop fusion | bytes 221188 | tf_op jit(solution)/shard_map/jit(dynamic_index_in_dim)/squeeze | solution.py:101
  7.3 0.0 copy-start.2
  7.4 1.0 %copy-done.2 = bf16[384,512]{1,0:T(8,128)(2,1)S(1)} copy-done((bf16[384,512]{1,0:T(8,128)(2,1)S(1)}, bf16[384,512]{1,0:T(8,128)(2,1)}, u32[]{:S(2)}) %copy-start.2) | copy-done | bytes 393240
  8.3 0.9 %shard_map.68 = (bf16[3,144,128]{2,1,0:T(8,128)(2,1)S(1)}, bf16[3,144,128]{2,1,0:T(8,128)(2,1)S(1)}, bf16[3,144,128]{2,1,0:T(8,128)(2,1)S(1)}, bf16[3,144,128]{2,1,0:T(8,128)(2,1)S(1)}) custom-call(f32[24,9216]{1,0:T(8,128)S(1)} %bitcast.5, f32[24,9216]{1,0:T(8,128)S(1)} %bitcast.6, bf16[384,512]{1,0:T(8,128)(2,1)S(1)} %copy-done.2, ...), custom_call_target="tpu_custom_call" | custom-call | tf_op jit(solution)/shard_map/pallas_call | solution.py:348
  9.2 0.1 collective-permute-start
  9.3 1.6 %collective-permute-start.1 = (bf16[3,144,128]{2,1,0:T(8,128)(2,1)S(1)}, bf16[3,144,128]{2,1,0:T(8,128)(2,1)S(1)}, u32[]{:S(2)}, u32[]{:S(2)}) collective-permute-start(bf16[3,144,128]{2,1,0:T(8,128)(2,1)S(1)} %get-tuple-element.50), channel_id=1, source_target_pairs={{0,2},{1,3},{2,0},{3,1},{4,6},{5,7},{6,4},{7,5},{8,10},{9,11},{10,... | collective-permute-start | bytes 331784 | tf_op jit(solution)/shard_map/ppermute | solution.py:366
  10.9 0.3 collective-permute-start.2
  11.2 6.9 %collective-permute-done.10.b_ref.refs_5_ = bf16[8,9216]{1,0:T(8,128)(2,1)S(1)} collective-permute-done((bf16[8,9216]{1,0:T(8,128)(2,1)S(1)}, bf16[8,9216]{1,0:T(8,128)(2,1)S(1)}, u32[]{:S(2)}, u32[]{:S(2)}) %collective-permute-start.10) | collective-permute-done | bytes 147488 | tf_op jit(solution)/shard_map/ppermute | solution.py:18
  18.1 0.0 collective-permute-done.6.b_ref.refs_5_
  18.1 0.8 %shard_map.72 = (bf16[3,96,128]{2,1,0:T(8,128)(2,1)S(1)}, bf16[3,96,128]{2,1,0:T(8,128)(2,1)S(1)}, bf16[3,96,128]{2,1,0:T(8,128)(2,1)S(1)}, bf16[3,96,128]{2,1,0:T(8,128)(2,1)S(1)}) custom-call(f32[24,9216]{1,0:T(8,128)S(1)} %bitcast.7, bf16[16,9216]{1,0:T(8,128)(2,1)S(1)} %collective-permute-done.6.b_ref.refs_5_, bf16[384,512]{1,0:T(8,128)(2,1)S(1)} %copy-done.2, ...), custom_call_target="tpu_custom_call" | custom-call | tf_op jit(solution)/shard_map/pallas_call | solution.py:348
  18.9 0.0 copy-start.4
  19.0 1.2 %shard_map.73 = (bf16[3,48,128]{2,1,0:T(8,128)(2,1)S(1)}, bf16[3,48,128]{2,1,0:T(8,128)(2,1)}, bf16[3,48,128]{2,1,0:T(8,128)(2,1)S(1)}, bf16[3,48,128]{2,1,0:T(8,128)(2,1)S(1)}) custom-call(f32[24,9216]{1,0:T(8,128)S(1)} %bitcast.8, bf16[8,9216]{1,0:T(8,128)(2,1)S(1)} %collective-permute-done.10.b_ref.refs_5_, bf16[384,512]{1,0:T(8,128)(2,1)S(1)} %copy-done.2, ...), custom_call_target="tpu_custom_call" | custom-call | tf_op jit(solution)/shard_map/pallas_call | solution.py:348
  20.1 0.6 %copy-done.5 = bf16[3,48,128]{2,1,0:T(8,128)(2,1)} copy-done((bf16[3,48,128]{2,1,0:T(8,128)(2,1)}, bf16[3,48,128]{2,1,0:T(8,128)(2,1)S(1)}, u32[]{:S(2)}) %copy-start.5) | copy-done | bytes 36888
  20.7 0.0 collective-permute-start.11
  20.7 0.5 collective-permute-start.7
  21.2 0.0 collective-permute-done.refs_1_
  21.2 1.5 %collective-permute-start.8 = (bf16[3,96,128]{2,1,0:T(8,128)(2,1)S(1)}, bf16[3,96,128]{2,1,0:T(8,128)(2,1)S(1)}, u32[]{:S(2)}, u32[]{:S(2)}) collective-permute-start(bf16[3,96,128]{2,1,0:T(8,128)(2,1)S(1)} %get-tuple-element.60), channel_id=1, source_target_pairs={{0,2},{1,3},{2,0},{3,1},{4,6},{5,7},{6,4},{7,5},{8,10},{9,11},{10,... | collective-permute-start | bytes 221192 | tf_op jit(solution)/shard_map/ppermute | solution.py:366
  22.7 0.0 collective-permute-done.1.refs_2_
  22.7 0.0 collective-permute-start.9
  22.7 0.0 collective-permute-done.2.refs_3_
  22.8 1.3 %collective-permute-start.12 = (bf16[3,48,128]{2,1,0:T(8,128)(2,1)}, bf16[3,48,128]{2,1,0:T(8,128)(2,1)S(1)}, u32[]{:S(2)}, u32[]{:S(2)}) collective-permute-start(bf16[3,48,128]{2,1,0:T(8,128)(2,1)} %copy-done.5), channel_id=1, source_target_pairs={{0,2},{1,3},{2,0},{3,1},{4,6},{5,7},{6,4},{7,5},{8,10},{9,11},{10,... | collective-permute-start | bytes 110600 | tf_op jit(solution)/shard_map/ppermute | solution.py:366
  24.1 0.0 collective-permute-done.11.refs_5_
  24.1 0.6 %collective-permute-start.13 = (bf16[3,48,128]{2,1,0:T(8,128)(2,1)S(1)}, bf16[3,48,128]{2,1,0:T(8,128)(2,1)S(1)}, u32[]{:S(2)}, u32[]{:S(2)}) collective-permute-start(bf16[3,48,128]{2,1,0:T(8,128)(2,1)S(1)} %get-tuple-element.68), channel_id=1, source_target_pairs={{0,3},{1,2},{2,1},{3,0},{4,7},{5,6},{6,5},{7,4},{8,11},{9,10},{10,... | collective-permute-start | bytes 110600 | tf_op jit(solution)/shard_map/ppermute | solution.py:366
  24.8 0.1 broadcast_in_dim.2.y_ref
  24.9 0.0 copy-done.4
  24.9 0.5 shard_map.69.refs_5_.refs_9_
  25.3 0.9 %shard_map.70 = (bf16[448,128]{1,0:T(8,128)(2,1)S(1)}, bf16[448,128]{1,0:T(8,128)(2,1)S(1)}, bf16[448,128]{1,0:T(8,128)(2,1)S(1)}, bf16[448,128]{1,0:T(8,128)(2,1)S(1)}) custom-call(bf16[3,144,128]{2,1,0:T(8,128)(2,1)S(1)} %get-tuple-element.48.refs_0_, bf16[3,144,128]{2,1,0:T(8,128)(2,1)S(1)} %collective-permute-done.refs_1_, ...), custom_call_target="tpu_custom_call" | custom-call | tf_op jit(solution)/shard_map/pallas_call | solution.py:348
  26.2 0.0 copy-start.3
  26.2 1.7 %collective-permute-done.12.refs_6_ = bf16[3,48,128]{2,1,0:T(8,128)(2,1)S(1)} collective-permute-done((bf16[3,48,128]{2,1,0:T(8,128)(2,1)}, bf16[3,48,128]{2,1,0:T(8,128)(2,1)S(1)}, u32[]{:S(2)}, u32[]{:S(2)}) %collective-permute-start.12) | collective-permute-done | bytes 36896 | tf_op jit(solution)/shard_map/ppermute | solution.py:366
  27.9 0.9 %collective-permute-done.13.refs_7_ = bf16[3,48,128]{2,1,0:T(8,128)(2,1)S(1)} collective-permute-done((bf16[3,48,128]{2,1,0:T(8,128)(2,1)S(1)}, bf16[3,48,128]{2,1,0:T(8,128)(2,1)S(1)}, u32[]{:S(2)}, u32[]{:S(2)}) %collective-permute-start.13) | collective-permute-done | bytes 36896 | tf_op jit(solution)/shard_map/ppermute | solution.py:366
  28.8 0.0 collective-permute-done.7.refs_1_
  28.8 0.0 collective-permute-done.8.refs_2_
  28.8 0.0 collective-permute-done.9.refs_3_
  28.8 0.9 %shard_map.74 = (bf16[304,128]{1,0:T(8,128)(2,1)S(1)}, bf16[304,128]{1,0:T(8,128)(2,1)S(1)}, bf16[304,128]{1,0:T(8,128)(2,1)S(1)}, bf16[304,128]{1,0:T(8,128)(2,...) custom-call(bf16[3,96,128]{2,1,0:T(8,128)(2,1)S(1)} %get-tuple-eleme, ...), custom_call_target="tpu_custom_call" | custom-call | tf_op jit(solution)/shard_map/pallas_call | solution.py:348
  29.7 0.1 collective-permute-start.14
  29.8 1.2 %collective-permute-start.15 = (bf16[304,128]{1,0:T(8,128)(2,1)S(1)}, bf16[304,128]{1,0:T(8,128)(2,1)S(1)}, u32[]{:S(2)}, u32[]{:S(2)}) collective-permute-start(bf16[304,128]{1,0:T(8,128)(2,1)S(1)} %get-tuple-element.79), channel_id=1, source_target_pairs={{0,2},{1,3},{2,0},{3,1},{4,6},{5,7},{6,4},{7,5},{8,10},{9,11},{10,... | collective-permute-start | bytes 233480 | tf_op jit(solution)/shard_map/ppermute | solution.py:366
  31.0 0.6 %collective-permute-start.16 = (bf16[304,128]{1,0:T(8,128)(2,1)S(1)}, bf16[304,128]{1,0:T(8,128)(2,1)S(1)}, u32[]{:S(2)}, u32[]{:S(2)}) collective-permute-start(bf16[304,128]{1,0:T(8,128)(2,1)S(1)} %get-tuple-element.80), channel_id=1, source_target_pairs={{0,3},{1,2},{2,1},{3,0},{4,7},{5,6},{6,5},{7,4},{8,11},{9,10},{10,... | collective-permute-start | bytes 233480 | tf_op jit(solution)/shard_map/ppermute | solution.py:366
  31.6 0.0 collective-permute-done.14.refs_1_
  31.6 3.4 %collective-permute-done.15.refs_2_ = bf16[304,128]{1,0:T(8,128)(2,1)S(1)} collective-permute-done((bf16[304,128]{1,0:T(8,128)(2,1)S(1)}, bf16[304,128]{1,0:T(8,128)(2,1)S(1)}, u32[]{:S(2)}, u32[]{:S(2)}) %collective-permute-start.15) | collective-permute-done | bytes 77856 | tf_op jit(solution)/shard_map/ppermute | solution.py:366
  35.0 0.6 %collective-permute-done.16.refs_3_ = bf16[304,128]{1,0:T(8,128)(2,1)S(1)} collective-permute-done((bf16[304,128]{1,0:T(8,128)(2,1)S(1)}, bf16[304,128]{1,0:T(8,128)(2,1)S(1)}, u32[]{:S(2)}, u32[]{:S(2)}) %collective-permute-start.16) | collective-permute-done | bytes 77856 | tf_op jit(solution)/shard_map/ppermute | solution.py:366
  35.6 0.0 copy-done.3
  35.6 0.7 %shard_map.75 = (f32[16,9216]{1,0:T(8,128)S(1)}, bf16[16,9344]{1,0:T(8,128)(2,1)S(1)}, f32[1,128]{1,0:T(1,128)S(1)}) custom-call(bf16[304,128]{1,0:T(8,128)(2,1)S(1)} %get-tuple-element.77.refs_0_, bf16[304,128]{1,0:T(8,128)(2,1)S(1)} %collective-permute-done.14.refs_1_, bf16[304,128]{1,0:T(8,128)(2,1)S(1)} %collective-permute-done.15.refs_2_, ...), custom_call_target="tpu_custom_call" | custom-call | tf_op jit(solution)/shard_map/pallas_call | solution.py:348
  36.4 1.8 %collective-permute-start.20 = (bf16[16,9344]{1,0:T(8,128)(2,1)S(1)}, bf16[16,9344]{1,0:T(8,128)(2,1)S(1)}, u32[]{:S(2)}, u32[]{:S(2)}) collective-permute-start(bf16[16,9344]{1,0:T(8,128)(2,1)S(1)} %get-tuple-element.90), channel_id=1, source_target_pairs={{0,28},{4,0},{8,4},{12,8},{16,12},{20,16},{24,20},{28,24},{1,29},{... | collective-permute-start | bytes 897032 | tf_op jit(solution)/shard_map/ppermute | solution.py:18
  38.2 0.1 collective-permute-start.17
  38.3 1.0 %collective-permute-start.18 = (bf16[144,128]{1,0:T(8,128)(2,1)S(1)}, bf16[144,128]{1,0:T(8,128)(2,1)S(1)}, u32[]{:S(2)}, u32[]{:S(2)}) collective-permute-start(bf16[144,128]{1,0:T(8,128)(2,1)S(1)} %get-tuple-element.84), channel_id=1, source_target_pairs={{0,2},{1,3},{2,0},{3,1},{4,6},{5,7},{6,4},{7,5},{8,10},{9,11},{10,... | collective-permute-start | bytes 110600 | tf_op jit(solution)/shard_map/ppermute | solution.py:366
  39.3 0.7 %collective-permute-start.19 = (bf16[144,128]{1,0:T(8,128)(2,1)S(1)}, bf16[144,128]{1,0:T(8,128)(2,1)S(1)}, u32[]{:S(2)}, u32[]{:S(2)}) collective-permute-start(bf16[144,128]{1,0:T(8,128)(2,1)S(1)} %get-tuple-element.85), channel_id=1, source_target_pairs={{0,3},{1,2},{2,1},{3,0},{4,7},{5,6},{6,5},{7,4},{8,11},{9,10},{10,... | collective-permute-start | bytes 110600 | tf_op jit(solution)/shard_map/ppermute | solution.py:366
  40.0 0.0 collective-permute-done.17.refs_1_
  40.0 2.2 %collective-permute-done.18.refs_2_ = bf16[144,128]{1,0:T(8,128)(2,1)S(1)} collective-permute-done((bf16[144,128]{1,0:T(8,128)(2,1)S(1)}, bf16[144,128]{1,0:T(8,128)(2,1)S(1)}, u32[]{:S(2)}, u32[]{:S(2)}) %collective-permute-start.18) | collective-permute-done | bytes 36896 | tf_op jit(solution)/shard_map/ppermute | solution.py:366
  42.2 0.7 %collective-permute-done.19.refs_3_ = bf16[144,128]{1,0:T(8,128)(2,1)S(1)} collective-permute-done((bf16[144,128]{1,0:T(8,128)(2,1)S(1)}, bf16[144,128]{1,0:T(8,128)(2,1)S(1)}, u32[]{:S(2)}, u32[]{:S(2)}) %collective-permute-start.19) | collective-permute-done | bytes 36896 | tf_op jit(solution)/shard_map/ppermute | solution.py:366
  42.9 0.5 shard_map.76
  43.4 1.5 %collective-permute-start.21 = (bf16[8,9216]{1,0:T(8,128)(2,1)S(1)}, bf16[8,9216]{1,0:T(8,128)(2,1)S(1)}, u32[]{:S(2)}, u32[]{:S(2)}) collective-permute-start(bf16[8,9216]{1,0:T(8,128)(2,1)S(1)} %get-tuple-element.91), channel_id=1, source_target_pairs={{0,28},{4,0},{8,4},{12,8},{16,12},{20,16},{24,20},{28,24},{1,29},{... | collective-permute-start | bytes 442376 | tf_op jit(solution)/shard_map/ppermute | solution.py:18
  44.8 0.0 collective-permute-start.3
  44.9 1.0 %collective-permute-start.4 = (bf16[448,128]{1,0:T(8,128)(2,1)S(1)}, bf16[448,128]{1,0:T(8,128)(2,1)S(1)}, u32[]{:S(2)}, u32[]{:S(2)}) collective-permute-start(bf16[448,128]{1,0:T(8,128)(2,1)S(1)} %get-tuple-element.54), channel_id=1, source_target_pairs={{0,2},{1,3},{2,0},{3,1},{4,6},{5,7},{6,4},{7,5},{8,10},{9,11},{10,... | collective-permute-start | bytes 344072 | tf_op jit(solution)/shard_map/ppermute | solution.py:366
  45.9 0.8 %collective-permute-start.5 = (bf16[448,128]{1,0:T(8,128)(2,1)S(1)}, bf16[448,128]{1,0:T(8,128)(2,1)S(1)}, u32[]{:S(2)}, u32[]{:S(2)}) collective-permute-start(bf16[448,128]{1,0:T(8,128)(2,1)S(1)} %get-tuple-element.55), channel_id=1, source_target_pairs={{0,3},{1,2},{2,1},{3,0},{4,7},{5,6},{6,5},{7,4},{8,11},{9,10},{10,... | collective-permute-start | bytes 344072 | tf_op jit(solution)/shard_map/ppermute | solution.py:366
  46.7 0.0 collective-permute-done.3.refs_1_
  46.7 4.2 %collective-permute-done.4.refs_2_ = bf16[448,128]{1,0:T(8,128)(2,1)S(1)} collective-permute-done((bf16[448,128]{1,0:T(8,128)(2,1)S(1)}, bf16[448,128]{1,0:T(8,128)(2,1)S(1)}, u32[]{:S(2)}, u32[]{:S(2)}) %collective-permute-start.4) | collective-permute-done | bytes 114720 | tf_op jit(solution)/shard_map/ppermute | solution.py:366
  50.9 1.5 %collective-permute-done.5.refs_3_ = bf16[448,128]{1,0:T(8,128)(2,1)S(1)} collective-permute-done((bf16[448,128]{1,0:T(8,128)(2,1)S(1)}, bf16[448,128]{1,0:T(8,128)(2,1)S(1)}, u32[]{:S(2)}, u32[]{:S(2)}) %collective-permute-start.5) | collective-permute-done | bytes 114720 | tf_op jit(solution)/shard_map/ppermute | solution.py:366
  52.4 0.8 %shard_map.77 = (f32[24,9216]{1,0:T(8,128)S(1)}, f32[1,128]{1,0:T(1,128)S(1)}) custom-call(bf16[448,128]{1,0:T(8,128)(2,1)S(1)} %get-tuple-element.52.refs_0_, bf16[448,128]{1,0:T(8,128)(2,1)S(1)} %collective-permute-done.3.refs_1_, bf16[448,128]{1,0:T(8,128)(2,1)S(1)} %collective-permute-done.4.refs_2_, ...), custom_call_target="tpu_custom_call" | custom-call | tf_op jit(solution)/shard_map/pallas_call | solution.py:348
  53.2 0.0 collective-permute-done.21.refs_1_
  53.2 0.0 collective-permute-done.20.refs_0_
  53.2 1.0 %last.1 = (f32[24,9216]{1,0:T(8,128)}, f32[1,1]{1,0:T(1,128)}) custom-call(f32[24,9216]{1,0:T(8,128)S(1)} %get-tuple-element.88.run_ref, f32[1,128]{1,0:T(1,128)S(1)} %get-tuple-element.89.sum_ref, bf16[16,9344]{1,0:T(8,128)(2,1)S(1)} %collective-permute-done.20.refs_0_, bf16[8,9216]{1,0:T(8,128)(2,1)S(1)} %collective-permute-done.21.refs_1_), custom_call_target="tpu_custom_call" | custom-call | tf_op jit(solution)/shard_map/last/pallas_call | solution.py:473
  (6 shorter events, 0.1 us)
Async XLA Ops:
  0.6 1.2 %copy-start = (f32[1,24,9216]{2,1,0:T(8,128)S(1)}, f32[1,24,9216]{2,1,0:T(8,128)}, u32[]{:S(2)}) copy-start(f32[1,24,9216]{2,1,0:T(8,128)} %param.5) | copy-start | bytes 2654212
  1.8 5.5 %copy-start.1 = (f32[1,24,9216]{2,1,0:T(8,128)S(1)}, f32[1,24,9216]{2,1,0:T(8,128)}, u32[]{:S(2)}) copy-start(f32[1,24,9216]{2,1,0:T(8,128)} %param.5) | copy-start | bytes 2654212
  1.8 16.3 %collective-permute-start.6 = (bf16[16,9216]{1,0:T(8,128)(2,1)S(1)}, bf16[16,9216]{1,0:T(8,128)(2,1)S(1)}, u32[]{:S(2)}, u32[]{:S(2)}) collective-permute-start(bf16[16,9216]{1,0:T(8,128)(2,1)S(1)} %get-tuple-element.56), channel_id=1, source_target_pairs={{0,4},{4,8},{8,12},{12,16},{16,20},{20,24},{24,28},{28,0},{1,5},{5... | collective-permute-start | bytes 884744 | tf_op jit(solution)/shard_map/ppermute | solution.py:18
  4.9 13.2 %collective-permute-start.10 = (bf16[8,9216]{1,0:T(8,128)(2,1)S(1)}, bf16[8,9216]{1,0:T(8,128)(2,1)S(1)}, u32[]{:S(2)}, u32[]{:S(2)}) collective-permute-start(bf16[8,9216]{1,0:T(8,128)(2,1)S(1)} %get-tuple-element.62), channel_id=1, source_target_pairs={{0,4},{4,8},{8,12},{12,16},{16,20},{20,24},{24,28},{28,0},{1,5},{5... | collective-permute-start | bytes 442376 | tf_op jit(solution)/shard_map/ppermute | solution.py:18
  7.3 1.0 %copy-start.2 = (bf16[384,512]{1,0:T(8,128)(2,1)S(1)}, bf16[384,512]{1,0:T(8,128)(2,1)}, u32[]{:S(2)}) copy-start(bf16[384,512]{1,0:T(8,128)(2,1)} %constant.24.clone.z_ref) | copy-start | bytes 1179652
  9.2 12.0 %collective-permute-start = (bf16[3,144,128]{2,1,0:T(8,128)(2,1)S(1)}, bf16[3,144,128]{2,1,0:T(8,128)(2,1)S(1)}, u32[]{:S(2)}, u32[]{:S(2)}) collective-permute-start(bf16[3,144,128]{2,1,0:T(8,128)(2,1)S(1)} %get-tuple-element.49), channel_id=1, source_target_pairs={{0,1},{1,0},{2,3},{3,2},{4,5},{5,4},{6,7},{7,6},{8,9},{9,8},{10,11... | collective-permute-start | bytes 331784 | tf_op jit(solution)/shard_map/ppermute | solution.py:366
  9.3 13.4 %collective-permute-start.1 = (bf16[3,144,128]{2,1,0:T(8,128)(2,1)S(1)}, bf16[3,144,128]{2,1,0:T(8,128)(2,1)S(1)}, u32[]{:S(2)}, u32[]{:S(2)}) collective-permute-start(bf16[3,144,128]{2,1,0:T(8,128)(2,1)S(1)} %get-tuple-element.50), channel_id=1, source_target_pairs={{0,2},{1,3},{2,0},{3,1},{4,6},{5,7},{6,4},{7,5},{8,10},{9,11},{10,... | collective-permute-start | bytes 331784 | tf_op jit(solution)/shard_map/ppermute | solution.py:366
  10.9 11.9 %collective-permute-start.2 = (bf16[3,144,128]{2,1,0:T(8,128)(2,1)S(1)}, bf16[3,144,128]{2,1,0:T(8,128)(2,1)S(1)}, u32[]{:S(2)}, u32[]{:S(2)}) collective-permute-start(bf16[3,144,128]{2,1,0:T(8,128)(2,1)S(1)} %get-tuple-element.51), channel_id=1, source_target_pairs={{0,3},{1,2},{2,1},{3,0},{4,7},{5,6},{6,5},{7,4},{8,11},{9,10},{10,... | collective-permute-start | bytes 331784 | tf_op jit(solution)/shard_map/ppermute | solution.py:366
  18.9 5.9 %copy-start.4 = (s32[96,2304]{1,0:T(8,128)S(1)}, s32[96,2304]{1,0:T(8,128)}, u32[]{:S(2)}) copy-start(s32[96,2304]{1,0:T(8,128)} %kept_ref.1) | copy-start | bytes 2654212
  20.1 0.6 %copy-start.5 = (bf16[3,48,128]{2,1,0:T(8,128)(2,1)}, bf16[3,48,128]{2,1,0:T(8,128)(2,1)S(1)}, u32[]{:S(2)}) copy-start(bf16[3,48,128]{2,1,0:T(8,128)(2,1)S(1)} %get-tuple-element.67) | copy-start | bytes 110596
  20.7 3.4 %collective-permute-start.11 = (bf16[3,48,128]{2,1,0:T(8,128)(2,1)}, bf16[3,48,128]{2,1,0:T(8,128)(2,1)S(1)}, u32[]{:S(2)}, u32[]{:S(2)}) collective-permute-start(bf16[3,48,128]{2,1,0:T(8,128)(2,1)} %get-tuple-element.66), channel_id=1, source_target_pairs={{0,1},{1,0},{2,3},{3,2},{4,5},{5,4},{6,7},{7,6},{8,9},{9,8},{10,11... | collective-permute-start | bytes 110600 | tf_op jit(solution)/shard_map/ppermute | solution.py:366
  20.7 8.1 %collective-permute-start.7 = (bf16[3,96,128]{2,1,0:T(8,128)(2,1)S(1)}, bf16[3,96,128]{2,1,0:T(8,128)(2,1)S(1)}, u32[]{:S(2)}, u32[]{:S(2)}) collective-permute-start(bf16[3,96,128]{2,1,0:T(8,128)(2,1)S(1)} %get-tuple-element.59), channel_id=1, source_target_pairs={{0,1},{1,0},{2,3},{3,2},{4,5},{5,4},{6,7},{7,6},{8,9},{9,8},{10,11... | collective-permute-start | bytes 221192 | tf_op jit(solution)/shard_map/ppermute | solution.py:366
  21.2 7.6 %collective-permute-start.8 = (bf16[3,96,128]{2,1,0:T(8,128)(2,1)S(1)}, bf16[3,96,128]{2,1,0:T(8,128)(2,1)S(1)}, u32[]{:S(2)}, u32[]{:S(2)}) collective-permute-start(bf16[3,96,128]{2,1,0:T(8,128)(2,1)S(1)} %get-tuple-element.60), channel_id=1, source_target_pairs={{0,2},{1,3},{2,0},{3,1},{4,6},{5,7},{6,4},{7,5},{8,10},{9,11},{10,... | collective-permute-start | bytes 221192 | tf_op jit(solution)/shard_map/ppermute | solution.py:366
  22.7 6.1 %collective-permute-start.9 = (bf16[3,96,128]{2,1,0:T(8,128)(2,1)S(1)}, bf16[3,96,128]{2,1,0:T(8,128)(2,1)S(1)}, u32[]{:S(2)}, u32[]{:S(2)}) collective-permute-start(bf16[3,96,128]{2,1,0:T(8,128)(2,1)S(1)} %get-tuple-element.61), channel_id=1, source_target_pairs={{0,3},{1,2},{2,1},{3,0},{4,7},{5,6},{6,5},{7,4},{8,11},{9,10},{10,... | collective-permute-start | bytes 221192 | tf_op jit(solution)/shard_map/ppermute | solution.py:366
  22.8 5.2 %collective-permute-start.12 = (bf16[3,48,128]{2,1,0:T(8,128)(2,1)}, bf16[3,48,128]{2,1,0:T(8,128)(2,1)S(1)}, u32[]{:S(2)}, u32[]{:S(2)}) collective-permute-start(bf16[3,48,128]{2,1,0:T(8,128)(2,1)} %copy-done.5), channel_id=1, source_target_pairs={{0,2},{1,3},{2,0},{3,1},{4,6},{5,7},{6,4},{7,5},{8,10},{9,11},{10,... | collective-permute-start | bytes 110600 | tf_op jit(solution)/shard_map/ppermute | solution.py:366
  24.1 4.7 %collective-permute-start.13 = (bf16[3,48,128]{2,1,0:T(8,128)(2,1)S(1)}, bf16[3,48,128]{2,1,0:T(8,128)(2,1)S(1)}, u32[]{:S(2)}, u32[]{:S(2)}) collective-permute-start(bf16[3,48,128]{2,1,0:T(8,128)(2,1)S(1)} %get-tuple-element.68), channel_id=1, source_target_pairs={{0,3},{1,2},{2,1},{3,0},{4,7},{5,6},{6,5},{7,4},{8,11},{9,10},{10,... | collective-permute-start | bytes 110600 | tf_op jit(solution)/shard_map/ppermute | solution.py:366
  26.2 9.4 %copy-start.3 = (bf16[512,384]{1,0:T(8,128)(2,1)S(1)}, bf16[512,384]{1,0:T(8,128)(2,1)}, u32[]{:S(2)}) copy-start(bf16[512,384]{1,0:T(8,128)(2,1)} %constant.25.clone.refs_6_.refs_8_) | copy-start | bytes 1179652
  29.7 1.9 %collective-permute-start.14 = (bf16[304,128]{1,0:T(8,128)(2,1)S(1)}, bf16[304,128]{1,0:T(8,128)(2,1)S(1)}, u32[]{:S(2)}, u32[]{:S(2)}) collective-permute-start(bf16[304,128]{1,0:T(8,128)(2,1)S(1)} %get-tuple-element.78), channel_id=1, source_target_pairs={{0,1},{1,0},{2,3},{3,2},{4,5},{5,4},{6,7},{7,6},{8,9},{9,8},{10,11... | collective-permute-start | bytes 233480 | tf_op jit(solution)/shard_map/ppermute | solution.py:366
  29.8 5.3 %collective-permute-start.15 = (bf16[304,128]{1,0:T(8,128)(2,1)S(1)}, bf16[304,128]{1,0:T(8,128)(2,1)S(1)}, u32[]{:S(2)}, u32[]{:S(2)}) collective-permute-start(bf16[304,128]{1,0:T(8,128)(2,1)S(1)} %get-tuple-element.79), channel_id=1, source_target_pairs={{0,2},{1,3},{2,0},{3,1},{4,6},{5,7},{6,4},{7,5},{8,10},{9,11},{10,... | collective-permute-start | bytes 233480 | tf_op jit(solution)/shard_map/ppermute | solution.py:366
  31.0 4.7 %collective-permute-start.16 = (bf16[304,128]{1,0:T(8,128)(2,1)S(1)}, bf16[304,128]{1,0:T(8,128)(2,1)S(1)}, u32[]{:S(2)}, u32[]{:S(2)}) collective-permute-start(bf16[304,128]{1,0:T(8,128)(2,1)S(1)} %get-tuple-element.80), channel_id=1, source_target_pairs={{0,3},{1,2},{2,1},{3,0},{4,7},{5,6},{6,5},{7,4},{8,11},{9,10},{10,... | collective-permute-start | bytes 233480 | tf_op jit(solution)/shard_map/ppermute | solution.py:366
  36.4 16.8 %collective-permute-start.20 = (bf16[16,9344]{1,0:T(8,128)(2,1)S(1)}, bf16[16,9344]{1,0:T(8,128)(2,1)S(1)}, u32[]{:S(2)}, u32[]{:S(2)}) collective-permute-start(bf16[16,9344]{1,0:T(8,128)(2,1)S(1)} %get-tuple-element.90), channel_id=1, source_target_pairs={{0,28},{4,0},{8,4},{12,8},{16,12},{20,16},{24,20},{28,24},{1,29},{... | collective-permute-start | bytes 897032 | tf_op jit(solution)/shard_map/ppermute | solution.py:18
  38.2 1.9 %collective-permute-start.17 = (bf16[144,128]{1,0:T(8,128)(2,1)S(1)}, bf16[144,128]{1,0:T(8,128)(2,1)S(1)}, u32[]{:S(2)}, u32[]{:S(2)}) collective-permute-start(bf16[144,128]{1,0:T(8,128)(2,1)S(1)} %get-tuple-element.83), channel_id=1, source_target_pairs={{0,1},{1,0},{2,3},{3,2},{4,5},{5,4},{6,7},{7,6},{8,9},{9,8},{10,11... | collective-permute-start | bytes 110600 | tf_op jit(solution)/shard_map/ppermute | solution.py:366
  38.3 4.0 %collective-permute-start.18 = (bf16[144,128]{1,0:T(8,128)(2,1)S(1)}, bf16[144,128]{1,0:T(8,128)(2,1)S(1)}, u32[]{:S(2)}, u32[]{:S(2)}) collective-permute-start(bf16[144,128]{1,0:T(8,128)(2,1)S(1)} %get-tuple-element.84), channel_id=1, source_target_pairs={{0,2},{1,3},{2,0},{3,1},{4,6},{5,7},{6,4},{7,5},{8,10},{9,11},{10,... | collective-permute-start | bytes 110600 | tf_op jit(solution)/shard_map/ppermute | solution.py:366
  39.3 3.6 %collective-permute-start.19 = (bf16[144,128]{1,0:T(8,128)(2,1)S(1)}, bf16[144,128]{1,0:T(8,128)(2,1)S(1)}, u32[]{:S(2)}, u32[]{:S(2)}) collective-permute-start(bf16[144,128]{1,0:T(8,128)(2,1)S(1)} %get-tuple-element.85), channel_id=1, source_target_pairs={{0,3},{1,2},{2,1},{3,0},{4,7},{5,6},{6,5},{7,4},{8,11},{9,10},{10,... | collective-permute-start | bytes 110600 | tf_op jit(solution)/shard_map/ppermute | solution.py:366
  43.4 9.8 %collective-permute-start.21 = (bf16[8,9216]{1,0:T(8,128)(2,1)S(1)}, bf16[8,9216]{1,0:T(8,128)(2,1)S(1)}, u32[]{:S(2)}, u32[]{:S(2)}) collective-permute-start(bf16[8,9216]{1,0:T(8,128)(2,1)S(1)} %get-tuple-element.91), channel_id=1, source_target_pairs={{0,28},{4,0},{8,4},{12,8},{16,12},{20,16},{24,20},{28,24},{1,29},{... | collective-permute-start | bytes 442376 | tf_op jit(solution)/shard_map/ppermute | solution.py:18
  44.8 1.9 %collective-permute-start.3 = (bf16[448,128]{1,0:T(8,128)(2,1)S(1)}, bf16[448,128]{1,0:T(8,128)(2,1)S(1)}, u32[]{:S(2)}, u32[]{:S(2)}) collective-permute-start(bf16[448,128]{1,0:T(8,128)(2,1)S(1)} %get-tuple-element.53), channel_id=1, source_target_pairs={{0,1},{1,0},{2,3},{3,2},{4,5},{5,4},{6,7},{7,6},{8,9},{9,8},{10,11... | collective-permute-start | bytes 344072 | tf_op jit(solution)/shard_map/ppermute | solution.py:366
  44.9 6.0 %collective-permute-start.4 = (bf16[448,128]{1,0:T(8,128)(2,1)S(1)}, bf16[448,128]{1,0:T(8,128)(2,1)S(1)}, u32[]{:S(2)}, u32[]{:S(2)}) collective-permute-start(bf16[448,128]{1,0:T(8,128)(2,1)S(1)} %get-tuple-element.54), channel_id=1, source_target_pairs={{0,2},{1,3},{2,0},{3,1},{4,6},{5,7},{6,4},{7,5},{8,10},{9,11},{10,... | collective-permute-start | bytes 344072 | tf_op jit(solution)/shard_map/ppermute | solution.py:366
  45.9 6.5 %collective-permute-start.5 = (bf16[448,128]{1,0:T(8,128)(2,1)S(1)}, bf16[448,128]{1,0:T(8,128)(2,1)S(1)}, u32[]{:S(2)}, u32[]{:S(2)}) collective-permute-start(bf16[448,128]{1,0:T(8,128)(2,1)S(1)} %get-tuple-element.55), channel_id=1, source_target_pairs={{0,3},{1,2},{2,1},{3,0},{4,7},{5,6},{6,5},{7,4},{8,11},{9,10},{10,... | collective-permute-start | bytes 344072 | tf_op jit(solution)/shard_map/ppermute | solution.py:366
